TPU v7x, 128 devices: a whole 4x4x4 slice. The times are simulated.
128 devices in a mesh: lon: 8 (over z, y_hi), lat: 16 (over y_lo, x, core).
Axes of the slice: x: 4, y: 4 (y_hi: 2, y_lo: 2; y = y_hi * 2 + y_lo), z: 4, core: 2. Of those that a mesh axis runs over, the one named last changes fastest.
Arguments:
- fields: float32 [4, 8, 1024, 3600], P(None, None, 'lat', 'lon'), may hold values from -6 to 6
- thickness: float32 [8], replicated, may hold values from 5 to 250
- cutoff: int32 [256], replicated, may hold values from 2 to 1800
- barotropic: float32 [3, 1024, 3600], P(None, 'lat', 'lon'), may hold values from -6 to 6
- land_sea: int32 [1024, 3600], P('lat', 'lon'), may hold values 0 or 1
Outputs:
- filtered_tracers: float32 [2, 8, 1024, 3600], P(None, None, 'lat', 'lon')
- velocity: float32 [2, 8, 1024, 3600], P(None, None, 'lat', 'lon')
- sea_level: float32 [1024, 3600], P('lat', 'lon')
Inputs may be any that keep to these rules, and one draw needn't show every extreme that they name: `cutoff`: each filtered row's highest kept wavenumber.
All inputs are finite; a program needn't handle non-finite values. No bound on the sum of `land_sea` on one device may be relied on, other than what follows from the above.
Results may differ from a plain program's by a relative error of at most 0.0003.
Values sent between devices are 32-bit elements; how exact they have to be, the bound alone decides.
A program may use at most 128 MiB of HBM per device.

v0:
```python
import math

import jax
import jax.numpy as jnp
from jax import lax
from jax.sharding import PartitionSpec as P

POLE_DEV = 2
SUB = 20


wave_coef = 0.65
highest = lax.Precision.HIGHEST


def with_halo(value, sides, width):
    for axis, dim in sides:
        devices, length = (lax.axis_size(axis), value.shape[dim])
        up = [(i, (i + 1) % devices) for i in range(devices)]
        down = [(j, i) for i, j in up]
        last = lax.slice_in_dim(value, length - width, length, axis=dim)
        initial = lax.slice_in_dim(value, 0, width, axis=dim)
        before = lax.ppermute(last, axis, up)
        after = lax.ppermute(initial, axis, down)
        value = jnp.concatenate([before, value, after], axis=dim)
    return value


def trig_tables(rows_len, cols_len, period):
    product = lax.broadcasted_iota(jnp.int32, (rows_len, cols_len), 0) * lax.broadcasted_iota(
        jnp.int32, (rows_len, cols_len), 1
    )
    angles = (product % period).astype(jnp.float32) * (2.0 * math.pi / period)
    return (jnp.cos(angles), jnp.sin(angles))


def spectral_cut(values, row_cuts):
    item_count, circle_len = values.shape
    first_len = max((d for d in range(1, math.isqrt(circle_len) + 1) if circle_len % d == 0))
    second_len = circle_len // first_len
    cos_first, sin_first = trig_tables(first_len, first_len, first_len)
    cos_second, sin_second = trig_tables(second_len, second_len, second_len)
    twist_cos, twist_sin = trig_tables(first_len, second_len, circle_len)
    grid = values.reshape(item_count, first_len, second_len)
    step_real = jnp.einsum("inb,nm->imb", grid, cos_first, precision=highest)
    step_imag = -jnp.einsum("inb,nm->imb", grid, sin_first, precision=highest)
    turn_real = step_real * twist_cos + step_imag * twist_sin
    turn_imag = step_imag * twist_cos - step_real * twist_sin
    spec_real = jnp.einsum("imb,bk->imk", turn_real, cos_second, precision=highest) + jnp.einsum(
        "imb,bk->imk", turn_imag, sin_second, precision=highest
    )
    spec_imag = jnp.einsum("imb,bk->imk", turn_imag, cos_second, precision=highest) - jnp.einsum(
        "imb,bk->imk", turn_real, sin_second, precision=highest
    )
    wavenumber = lax.broadcasted_iota(
        jnp.int32, (first_len, second_len), 0
    ) + first_len * lax.broadcasted_iota(jnp.int32, (first_len, second_len), 1)
    folded = jnp.minimum(wavenumber, circle_len - wavenumber)
    kept_mask = jnp.where(folded[None, :, :] <= row_cuts[:, None, None], 1.0 / circle_len, 0.0)
    spec_real = spec_real * kept_mask
    spec_imag = spec_imag * kept_mask
    part_real = jnp.einsum("imq,qk->imk", spec_real, cos_second, precision=highest) - jnp.einsum(
        "imq,qk->imk", spec_imag, sin_second, precision=highest
    )
    part_imag = jnp.einsum("imq,qk->imk", spec_real, sin_second, precision=highest) + jnp.einsum(
        "imq,qk->imk", spec_imag, cos_second, precision=highest
    )
    back_real = part_real * twist_cos - part_imag * twist_sin
    back_imag = part_real * twist_sin + part_imag * twist_cos
    rebuilt = jnp.einsum("imk,mj->ijk", back_real, cos_first, precision=highest) - jnp.einsum(
        "imk,mj->ijk", back_imag, sin_first, precision=highest
    )
    return rebuilt.reshape(item_count, circle_len)


def row_cutoffs(cutoff, band, item_ids, band_rows, total_rows):
    pole_rows = cutoff.shape[0] // 2
    global_row = band * band_rows + item_ids % band_rows
    table_index = jnp.where(
        global_row < pole_rows, global_row, global_row - (total_rows - 2 * pole_rows)
    )
    matches = table_index[:, None] == lax.broadcasted_iota(jnp.int32, (1, 2 * pole_rows), 1)
    return jnp.sum(jnp.where(matches, cutoff[None, :], 0), axis=1)


def body(fields, thickness, cutoff, barotropic, land_sea):
    lon_count = lax.axis_size("lon")
    lat_count = lax.axis_size("lat")
    lat_index = lax.axis_index("lat")
    lon_index = lax.axis_index("lon")
    components, levels, band_rows, tile_cols = fields.shape
    total_rows = band_rows * lat_count
    total_items = components * levels * band_rows
    share_items = total_items // lon_count
    flattened = fields.reshape(total_items, tile_cols)
    circled = lax.all_to_all(flattened, "lon", split_axis=0, concat_axis=1, tiled=True)
    item_ids = lon_index * share_items + lax.iota(jnp.int32, share_items)
    north_pole = lat_index < POLE_DEV
    south_pole = lat_index >= lat_count - POLE_DEV
    row_cuts = row_cutoffs(cutoff, lat_index, item_ids, band_rows, total_rows)
    result = lax.cond(
        north_pole | south_pole,
        lambda values: spectral_cut(values, row_cuts),
        lambda values: values,
        circled,
    )
    returned = lax.all_to_all(result, "lon", split_axis=1, concat_axis=0, tiled=True)
    filtered = returned.reshape(components, levels, band_rows, tile_cols)
    rim_width = 4
    mask_wide = with_halo(land_sea, (("lon", 1), ("lat", 0)), rim_width + 1)
    ocean_wide = mask_wide.astype(jnp.float32)
    pad_rows = (
        lat_index * band_rows - rim_width - 1 + lax.iota(jnp.int32, band_rows + 2 * rim_width + 2)
    ) % total_rows
    east_wide = ocean_wide * jnp.roll(ocean_wide, -1, 1)
    north_wide = (
        ocean_wide
        * jnp.roll(ocean_wide, -1, 0)
        * (pad_rows != total_rows - 1).astype(jnp.float32)[:, None]
    )
    ocean_pad = ocean_wide[1:-1, 1:-1]
    east_pad = east_wide[1:-1, 1:-1]
    north_pad = north_wide[1:-1, 1:-1]

    def advance(cycle_index, state_now):
        padded = with_halo(state_now, (("lon", 2), ("lat", 1)), rim_width)
        surface = padded[0]
        eastward = padded[1] * east_pad
        northward = padded[2] * north_pad
        for subcycle in range(rim_width):
            divergence = eastward - jnp.roll(eastward, 1, 1) + northward - jnp.roll(northward, 1, 0)
            surface = surface - wave_coef * ocean_pad * divergence
            eastward = east_pad * (eastward - wave_coef * (jnp.roll(surface, -1, 1) - surface))
            northward = north_pad * (northward - wave_coef * (jnp.roll(surface, -1, 0) - surface))
        return jnp.stack([surface, eastward, northward])[
            :, rim_width:-rim_width, rim_width:-rim_width
        ]

    final_state = lax.fori_loop(0, SUB // rim_width, advance, barotropic)
    east_mid = east_pad[rim_width:-rim_width, rim_width:-rim_width]
    north_mid = north_pad[rim_width:-rim_width, rim_width:-rim_width]
    weights = thickness / jnp.sum(thickness)
    currents = filtered[2:]
    column = jnp.einsum("k,ckij->cij", weights, currents, precision=highest)
    velocity = jnp.stack([east_mid, north_mid])[:, None] * (
        currents - column[:, None] + final_state[1:][:, None]
    )
    return (filtered[:2], velocity, final_state[0])


def solution(mesh):
    return jax.shard_map(
        body,
        mesh=mesh,
        in_specs=(P(None, None, "lat", "lon"), P(), P(), P(None, "lat", "lon"), P("lat", "lon")),
        out_specs=(P(None, None, "lat", "lon"), P(None, None, "lat", "lon"), P("lat", "lon")),
        check_vma=False,
    )
```

profile of v0, /device:TPU:0, one launch (start us, length us, event | category | flops | bytes accessed | tf_op | source)
XLA Modules:
  0.0 315.3 jit_solution(11312199765640784743)
XLA Ops:
  0.6 5.3 %copy.115 = f32[8,256,450]{1,2,0:T(8,128)} copy(f32[8,256,450]{2,1,0:T(8,128)} %bitcast.272) | data formatting | bytes 7372800 | tf_op jit(solution)/shard_map/all_to_all | solution.py:96
  5.9 8.2 %all-to-all-start = ((f32[8,256,450]{1,2,0:T(8,128)}), f32[8,256,450]{1,2,0:T(8,128)}, u32[]{:S(2)}, u32[]{:S(2)}) async-start(f32[8,256,450]{1,2,0:T(8,128)} %copy.115), calls=%async_computation | async-start | bytes 7471104 | tf_op jit(solution)/shard_map/all_to_all | solution.py:96
  14.2 3.5 %collective-permute-start.4 = (s32[64,5]{1,0:T(8,128)S(1)}, s32[64,5]{1,0:T(8,128)S(1)}, u32[]{:S(2)}, u32[]{:S(2)}) collective-permute-start(s32[64,5]{1,0:T(8,128)S(1)} %get-tuple-element.334), channel_id=1, source_target_pairs={{0,16},{16,32},{32,48},{48,64},{64,80},{80,96},{96,112},{112,0},{1... | collective-permute-start | bytes 3848 | tf_op jit(solution)/shard_map/ppermute | solution.py:23
  17.7 2.2 collective-permute-start.5
  19.9 41.3 %collective-permute-done.4 = s32[64,5]{1,0:T(8,128)S(1)} collective-permute-done((s32[64,5]{1,0:T(8,128)S(1)}, s32[64,5]{1,0:T(8,128)S(1)}, u32[]{:S(2)}, u32[]{:S(2)}) %collective-permute-start.4) | collective-permute-done | bytes 1312 | tf_op jit(solution)/shard_map/ppermute | solution.py:23
  61.3 3.8 %collective-permute-start.7 = (s32[5,460]{1,0:T(8,128)S(1)}, s32[5,460]{1,0:T(8,128)S(1)}, u32[]{:S(2)}, u32[]{:S(2)}) collective-permute-start(s32[5,460]{1,0:T(8,128)S(1)} %get-tuple-element.331), channel_id=1, source_target_pairs={{1,0},{2,1},{3,2},{4,3},{5,4},{6,5},{7,6},{8,7},{9,8},{10,9},{11,1... | collective-permute-start | bytes 27608 | tf_op jit(solution)/shard_map/ppermute | solution.py:24
  65.2 0.6 reduce_sum.23
  65.8 0.8 collective-permute-done.6
  67.4 3.6 %all_to_all.32 = f32[256,3600]{0,1:T(8,128)} reshape(f32[256,8,450]{0,2,1:T(8,128)} %bitcast.39) | data formatting | bytes 7372800 | tf_op jit(solution)/shard_map/all_to_all | solution.py:96
  71.0 88.4 %conditional.1 = (f32[256,3600]{0,1:T(8,128)}) conditional(s32[]{:T(128)} %convert_element_type.71, f32[256,3600]{0,1:T(8,128)} %all_to_all.32, (f32[256,3600]{0,1:T(8,128)}, s32[]{:T(128)}, s32[]{:T(128)}, s32[256,1]{0,1:T(1,128)S(1)}, s32[]{:T(128)}, /*index=5*/s32[256,256]{1,0:T(8,128)S(1)}, s32[256]{0:T(256)S(1)}) %tuple.175), branch_computations={%region_0.1_spmd, %region_1.3_spmd.clone.clone} | conditional | flops 7985373696 | bytes 159001056 | solution.py:101
  71.8 4.9 %reshape.244 = f32[256,60,60]{0,2,1:T(8,128)} reshape(f32[256,3600]{0,1:T(8,128)} %get-tuple-element.223) | data formatting | bytes 7372800 | tf_op jit(solution)/shard_map/cond/branch_1_fun/reshape | solution.py:44
  76.7 8.0 %fusion.86 = f32[60,256,60]{1,0,2:T(8,128)S(1)} fusion(f32[256,60,60]{0,2,1:T(8,128)} %reshape.244), kind=kOutput, calls=%fused_computation.157 | convolution fusion | flops 663584384 | bytes 7372800 | tf_op jit(solution)/shard_map/cond/branch_1_fun/inb,nm->imb/dot_general | solution.py:46
  84.8 7.8 %add_bitcast_fusion = (f32[256,60,60]{0,1,2:T(8,128)S(1)}, f32[256,60,60]{0,1,2:T(8,128)S(1)}) fusion(f32[60,256,60]{1,0,2:T(8,128)S(1)} %fusion.86, f32[60,60]{0,1:T(8,128)S(1)} %get-tuple-element.258, f32[60,60]{0,1:T(8,128)S(1)} %get-tuple-element.259, f32[256,60,60]{0,2,1:T(8,128)S(1)} %copy-done.1), kind=kOutput, calls=%fused_computation.148 | convolution fusion | flops 670035584 | bytes 14774400 | tf_op jit(solution)/shard_map/cond/branch_1_fun/inb,nm->imb/dot_general | solution.py:45
  92.5 6.2 %fusion.78 = f32[256,60,60]{0,2,1:T(8,128)S(1)} fusion(f32[256,60,60]{0,1,2:T(8,128)S(1)} %get-tuple-element.257), kind=kOutput, calls=%fused_computation.149 | convolution fusion | flops 663584384 | bytes 7372800 | tf_op jit(solution)/shard_map/cond/branch_1_fun/imb,bk->imk/dot_general | solution.py:52
  98.8 7.7 %select_multiply_fusion = f32[256,60,60]{0,2,1:T(8,128)S(1)} fusion(f32[256,60,60]{0,2,1:T(8,128)S(1)} %fusion.78, f32[256,60,60]{0,1,2:T(8,128)S(1)} %get-tuple-element.256, s32[256]{0:T(256)S(1)} %select_reduce_fusion, s32[60,60]{1,0:T(8,128)S(1)} %copy.124), kind=kOutput, calls=%fused_computation.138 | convolution fusion | flops 667270784 | bytes 11074624 | tf_op jit(solution)/shard_map/cond/branch_1_fun/imb,bk->imk/dot_general | solution.py:52
  106.5 6.2 %fusion.80 = f32[256,60,60]{0,2,1:T(8,128)S(1)} fusion(f32[256,60,60]{0,1,2:T(8,128)S(1)} %get-tuple-element.257), kind=kOutput, calls=%fused_computation.151 | convolution fusion | flops 663584384 | bytes 7372800 | tf_op jit(solution)/shard_map/cond/branch_1_fun/imb,bk->imk/dot_general | solution.py:49
  112.7 7.4 %select_multiply_fusion.1 = f32[256,60,60]{0,2,1:T(8,128)S(1)} fusion(f32[256,60,60]{0,2,1:T(8,128)S(1)} %fusion.80, f32[256,60,60]{0,1,2:T(8,128)S(1)} %get-tuple-element.256, s32[256]{0:T(256)S(1)} %select_reduce_fusion, s32[60,60]{1,0:T(8,128)S(1)} %copy.124), kind=kOutput, calls=%fused_computation.139 | convolution fusion | flops 667270784 | bytes 11074624 | tf_op jit(solution)/shard_map/cond/branch_1_fun/imb,bk->imk/dot_general | solution.py:49
  120.1 3.9 %fusion.101 = f32[256,60,60]{0,2,1:T(8,128)S(1)} fusion(f32[256,60,60]{0,2,1:T(8,128)S(1)} %select_multiply_fusion.1), kind=kOutput, calls=%fused_computation.172 | convolution fusion | flops 663584384 | bytes 7372800 | tf_op jit(solution)/shard_map/cond/branch_1_fun/imq,qk->imk/dot_general | solution.py:65
  124.1 3.9 %fusion.110 = f32[256,60,60]{0,2,1:T(8,128)S(1)} fusion(f32[256,60,60]{0,2,1:T(8,128)S(1)} %select_multiply_fusion.1), kind=kOutput, calls=%fused_computation.181 | convolution fusion | flops 663584384 | bytes 7372800 | tf_op jit(solution)/shard_map/cond/branch_1_fun/imq,qk->imk/dot_general | solution.py:62
  128.0 4.2 %convolution_subtract_fusion = f32[256,60,60]{0,2,1:T(8,128)S(1)} fusion(f32[256,60,60]{0,2,1:T(8,128)S(1)} %fusion.110, f32[256,60,60]{0,2,1:T(8,128)S(1)} %select_multiply_fusion), kind=kOutput, calls=%fused_computation.162 | convolution fusion | flops 664505984 | bytes 11059200 | tf_op jit(solution)/shard_map/cond/branch_1_fun/imq,qk->imk/dot_general | solution.py:62
  132.2 6.1 %multiply_subtract_fusion = (f32[256,60,60]{0,2,1:T(8,128)S(1)}, f32[256,60,60]{0,2,1:T(8,128)S(1)}) fusion(f32[256,60,60]{0,2,1:T(8,128)S(1)} %convolution_subtract_fusion, f32[60,60]{1,0:T(8,128)S(1)} %copy.126, f32[60,60]{1,0:T(8,128)S(1)} %copy.125, f32[256,60,60]{0,2,1:T(8,128)S(1)} %fusion.101, f32[256,60,60]{0,2,1:T(8,128)S(1)} %select_multiply_fusion), kind=kOutput, calls=%fused_computation.146 | convolution fusion | flops 670035584 | bytes 18460800 | tf_op jit(solution)/shard_map/cond/branch_1_fun/imq,qk->imk/dot_general | solution.py:65
  138.3 5.8 %fusion.74 = f32[60,256,60]{1,0,2:T(8,128)S(1)} fusion(f32[256,60,60]{0,2,1:T(8,128)S(1)} %get-tuple-element.255), kind=kOutput, calls=%fused_computation.140 | convolution fusion | flops 663584384 | bytes 7372800 | tf_op jit(solution)/shard_map/cond/branch_1_fun/imk,mj->ijk/dot_general | solution.py:70
  144.1 6.3 %subtract_bitcast_fusion = f32[256,60,60]{0,1,2:T(8,128)S(1)} fusion(f32[60,256,60]{1,0,2:T(8,128)S(1)} %fusion.74, f32[256,60,60]{0,2,1:T(8,128)S(1)} %get-tuple-element.254), kind=kOutput, calls=%fused_computation.144 | convolution fusion | flops 664505984 | bytes 11059200 | tf_op jit(solution)/shard_map/cond/branch_1_fun/imk,mj->ijk/dot_general | solution.py:70
  150.4 4.0 %copy.129 = f32[256,60,60]{0,2,1:T(8,128)} copy(f32[256,60,60]{0,1,2:T(8,128)S(1)} %subtract_bitcast_fusion) | data formatting | bytes 7372800 | tf_op jit(solution)/shard_map/cond/branch_1_fun/sub | solution.py:70
  154.4 4.8 %reshape.245 = f32[256,3600]{0,1:T(8,128)} reshape(f32[256,60,60]{0,2,1:T(8,128)} %copy.129) | data formatting | bytes 7372800 | tf_op jit(solution)/shard_map/cond/branch_1_fun/reshape | solution.py:73
  159.4 3.6 %all_to_all.33 = f32[256,8,450]{0,2,1:T(8,128)} reshape(f32[256,3600]{0,1:T(8,128)} %get-tuple-element.537) | data formatting | bytes 7372800 | tf_op jit(solution)/shard_map/all_to_all | solution.py:107
  162.9 4.6 %all-to-all-start.1 = ((f32[256,8,450]{0,2,1:T(8,128)}), f32[256,8,450]{0,2,1:T(8,128)}, u32[]{:S(2)}, u32[]{:S(2)}) async-start(f32[256,8,450]{0,2,1:T(8,128)} %all_to_all.33), calls=%async_computation.1 | async-start | bytes 7471104 | tf_op jit(solution)/shard_map/all_to_all | solution.py:107
  167.6 132.5 %while.10 = (s32[]{:T(128)}, f32[3,64,450]{2,1,0:T(8,128)S(1)}, f32[72,458]{1,0:T(8,128)S(1)}, f32[72,458]{1,0:T(8,128)S(1)}, f32[72,458]{1,0:T(8,128)S(1)}, /*index=5*/s32[]{:T(128)}) while((s32[]{:T(128)}, f32[3,64,450]{2,1,0:T(8,128)S(1)}, f32[72,458]{1,0:T(8,128)S(1)}, f32[72,458]{1,0:T(8,128)S(1)}, f32[72,458]{1,0:T(8,128)S(1)}, ...), condition=%wide.region_5.6_spmd, body=%wide.region_4.5_spmd.sunk | while | flops 5437970 | bytes 21927012 | solution.py:139
  167.7 5.6 %collective-permute-start = (f32[3,64,4]{2,1,0:T(8,128)S(1)}, f32[3,64,4]{2,1,0:T(8,128)S(1)}, u32[]{:S(2)}, u32[]{:S(2)}) collective-permute-start(f32[3,64,4]{2,1,0:T(8,128)S(1)} %get-tuple-element.444), channel_id=1, source_target_pairs={{16,0},{32,16},{48,32},{64,48},{80,64},{96,80},{112,96},{0,112},{1... | collective-permute-start | bytes 9224 | tf_op jit(solution)/shard_map/while/body/eval_jaxpr/ppermute | solution.py:24
  173.3 42.6 %collective-permute-done = f32[3,64,4]{2,1,0:T(8,128)S(1)} collective-permute-done((f32[3,64,4]{2,1,0:T(8,128)S(1)}, f32[3,64,4]{2,1,0:T(8,128)S(1)}, u32[]{:S(2)}, u32[]{:S(2)}) %collective-permute-start) | collective-permute-done | bytes 3104 | tf_op jit(solution)/shard_map/while/body/eval_jaxpr/ppermute | solution.py:24
  215.9 2.0 collective-permute-done.1
  218.1 1.4 collective-permute-start.2
  219.5 1.5 collective-permute-done.2
  221.0 3.8 %collective-permute-done.3 = f32[3,4,458]{2,1,0:T(4,128)S(1)} collective-permute-done((f32[3,4,458]{2,1,0:T(4,128)S(1)}, f32[3,4,458]{2,1,0:T(4,128)S(1)}, u32[]{:S(2)}, u32[]{:S(2)}) %collective-permute-start.3) | collective-permute-done | bytes 22016 | tf_op jit(solution)/shard_map/while/body/eval_jaxpr/ppermute | solution.py:23
  228.3 1.3 collective-permute-start
  229.6 2.3 collective-permute-start.1
  231.9 2.6 collective-permute-done
  234.5 3.4 %collective-permute-done.1 = f32[3,64,4]{2,1,0:T(8,128)S(1)} collective-permute-done((f32[3,64,4]{2,1,0:T(8,128)S(1)}, f32[3,64,4]{2,1,0:T(8,128)S(1)}, u32[]{:S(2)}, u32[]{:S(2)}) %collective-permute-start.1) | collective-permute-done | bytes 3104 | tf_op jit(solution)/shard_map/while/body/eval_jaxpr/ppermute | solution.py:23
  238.0 0.5 collective-permute-start.3
  238.5 1.0 collective-permute-done.2
  239.6 3.9 %collective-permute-done.3 = f32[3,4,458]{2,1,0:T(4,128)S(1)} collective-permute-done((f32[3,4,458]{2,1,0:T(4,128)S(1)}, f32[3,4,458]{2,1,0:T(4,128)S(1)}, u32[]{:S(2)}, u32[]{:S(2)}) %collective-permute-start.3) | collective-permute-done | bytes 22016 | tf_op jit(solution)/shard_map/while/body/eval_jaxpr/ppermute | solution.py:23
  246.9 1.1 collective-permute-start
  248.0 2.5 collective-permute-start.1
  250.5 2.6 collective-permute-done
  253.1 3.2 %collective-permute-done.1 = f32[3,64,4]{2,1,0:T(8,128)S(1)} collective-permute-done((f32[3,64,4]{2,1,0:T(8,128)S(1)}, f32[3,64,4]{2,1,0:T(8,128)S(1)}, u32[]{:S(2)}, u32[]{:S(2)}) %collective-permute-start.1) | collective-permute-done | bytes 3104 | tf_op jit(solution)/shard_map/while/body/eval_jaxpr/ppermute | solution.py:23
  256.4 0.5 collective-permute-start.3
  256.9 1.0 collective-permute-done.2
  258.0 3.9 %collective-permute-done.3 = f32[3,4,458]{2,1,0:T(4,128)S(1)} collective-permute-done((f32[3,4,458]{2,1,0:T(4,128)S(1)}, f32[3,4,458]{2,1,0:T(4,128)S(1)}, u32[]{:S(2)}, u32[]{:S(2)}) %collective-permute-start.3) | collective-permute-done | bytes 22016 | tf_op jit(solution)/shard_map/while/body/eval_jaxpr/ppermute | solution.py:23
  265.4 3.5 %collective-permute-start.1 = (f32[3,64,4]{2,1,0:T(8,128)S(1)}, f32[3,64,4]{2,1,0:T(8,128)S(1)}, u32[]{:S(2)}, u32[]{:S(2)}) collective-permute-start(f32[3,64,4]{2,1,0:T(8,128)S(1)} %get-tuple-element.445), channel_id=1, source_target_pairs={{0,16},{16,32},{32,48},{48,64},{64,80},{80,96},{96,112},{112,0},{1... | collective-permute-start | bytes 9224 | tf_op jit(solution)/shard_map/while/body/eval_jaxpr/ppermute | solution.py:23
  268.9 2.6 collective-permute-done
  271.5 2.2 collective-permute-done.1
  274.4 1.0 collective-permute-done.2
  275.4 3.9 %collective-permute-done.3 = f32[3,4,458]{2,1,0:T(4,128)S(1)} collective-permute-done((f32[3,4,458]{2,1,0:T(4,128)S(1)}, f32[3,4,458]{2,1,0:T(4,128)S(1)}, u32[]{:S(2)}, u32[]{:S(2)}) %collective-permute-start.3) | collective-permute-done | bytes 22016 | tf_op jit(solution)/shard_map/while/body/eval_jaxpr/ppermute | solution.py:23
  282.8 3.5 %collective-permute-start.1 = (f32[3,64,4]{2,1,0:T(8,128)S(1)}, f32[3,64,4]{2,1,0:T(8,128)S(1)}, u32[]{:S(2)}, u32[]{:S(2)}) collective-permute-start(f32[3,64,4]{2,1,0:T(8,128)S(1)} %get-tuple-element.445), channel_id=1, source_target_pairs={{0,16},{16,32},{32,48},{48,64},{64,80},{80,96},{96,112},{112,0},{1... | collective-permute-start | bytes 9224 | tf_op jit(solution)/shard_map/while/body/eval_jaxpr/ppermute | solution.py:23
  286.3 2.6 collective-permute-done
  288.9 2.2 collective-permute-done.1
  291.8 1.0 collective-permute-done.2
  292.8 3.9 %collective-permute-done.3 = f32[3,4,458]{2,1,0:T(4,128)S(1)} collective-permute-done((f32[3,4,458]{2,1,0:T(4,128)S(1)}, f32[3,4,458]{2,1,0:T(4,128)S(1)}, u32[]{:S(2)}, u32[]{:S(2)}) %collective-permute-start.3) | collective-permute-done | bytes 22016 | tf_op jit(solution)/shard_map/while/body/eval_jaxpr/ppermute | solution.py:23
  300.2 0.7 slice_bitcast_fusion.34
  300.9 4.2 %fusion.225 = (f32[4,256,450]{1,2,0:T(8,128)}, f32[4,256,450]{1,2,0:T(8,128)}) fusion(f32[8,256,450]{1,2,0:T(8,128)} %bitcast.40), kind=kLoop, calls=%fused_computation.289 | loop fusion | bytes 7372800 | tf_op jit(solution)/shard_map/slice | solution.py:143
  305.1 1.9 copy.117
  307.0 3.4 %fusion.212 = f32[1,2,64,450]{3,0,2,1:T(1,128)S(1)} fusion(f32[2,8,64,450]{3,2,1,0:T(8,128)S(1)} %bitcast.270, f32[8]{0:T(128)S(1)} %copy-done.4, f32[]{:T(128)} %reduce_sum.23), kind=kOutput, calls=%fused_computation.265 | convolution fusion | flops 5529608 | bytes 2073636 | tf_op jit(solution)/shard_map/k,ckij->cij/dot_general | solution.py:144
  310.4 2.8 copy.116
  313.3 1.9 add_multiply_fusion
  (286 shorter events, 19.4 us)
Async XLA Ops:
  5.9 8.2 %copy-start.2 = (s32[64,450]{1,0:T(8,128)S(1)}, s32[64,450]{1,0:T(8,128)}, u32[]{:S(2)}) copy-start(s32[64,450]{1,0:T(8,128)} %param.13) | copy-start | bytes 345604
  5.9 59.3 %copy-start.4 = (f32[8]{0:T(128)S(1)}, f32[8]{0:T(128)}, u32[]{:S(2)}) copy-start(f32[8]{0:T(128)} %param.10) | copy-start | bytes 100
  5.9 61.4 %all-to-all-start = ((f32[8,256,450]{1,2,0:T(8,128)}), f32[8,256,450]{1,2,0:T(8,128)}, u32[]{:S(2)}, u32[]{:S(2)}) async-start(f32[8,256,450]{1,2,0:T(8,128)} %copy.115), calls=%async_computation | async-start | bytes 7471104 | tf_op jit(solution)/shard_map/all_to_all | solution.py:96
  14.2 47.0 %collective-permute-start.4 = (s32[64,5]{1,0:T(8,128)S(1)}, s32[64,5]{1,0:T(8,128)S(1)}, u32[]{:S(2)}, u32[]{:S(2)}) collective-permute-start(s32[64,5]{1,0:T(8,128)S(1)} %get-tuple-element.334), channel_id=1, source_target_pairs={{0,16},{16,32},{32,48},{48,64},{64,80},{80,96},{96,112},{112,0},{1... | collective-permute-start | bytes 3848 | tf_op jit(solution)/shard_map/ppermute | solution.py:23
  17.7 43.5 %collective-permute-start.5 = (s32[64,5]{1,0:T(8,128)S(1)}, s32[64,5]{1,0:T(8,128)S(1)}, u32[]{:S(2)}, u32[]{:S(2)}) collective-permute-start(s32[64,5]{1,0:T(8,128)S(1)} %get-tuple-element.335), channel_id=1, source_target_pairs={{16,0},{32,16},{48,32},{64,48},{80,64},{96,80},{112,96},{0,112},{1... | collective-permute-start | bytes 3848 | tf_op jit(solution)/shard_map/ppermute | solution.py:24
  61.3 5.3 %collective-permute-start.6 = (s32[5,460]{1,0:T(8,128)S(1)}, s32[5,460]{1,0:T(8,128)S(1)}, u32[]{:S(2)}, u32[]{:S(2)}) collective-permute-start(s32[5,460]{1,0:T(8,128)S(1)} %get-tuple-element.330), channel_id=1, source_target_pairs={{0,1},{1,2},{2,3},{3,4},{4,5},{5,6},{6,7},{7,8},{8,9},{9,10},{10,1... | collective-permute-start | bytes 27608 | tf_op jit(solution)/shard_map/ppermute | solution.py:23
  61.3 5.3 %collective-permute-start.7 = (s32[5,460]{1,0:T(8,128)S(1)}, s32[5,460]{1,0:T(8,128)S(1)}, u32[]{:S(2)}, u32[]{:S(2)}) collective-permute-start(s32[5,460]{1,0:T(8,128)S(1)} %get-tuple-element.331), channel_id=1, source_target_pairs={{1,0},{2,1},{3,2},{4,3},{5,4},{6,5},{7,6},{8,7},{9,8},{10,9},{11,1... | collective-permute-start | bytes 27608 | tf_op jit(solution)/shard_map/ppermute | solution.py:24
  67.3 3.7 %copy-start.3 = (s32[256]{0:T(256)S(1)}, s32[256]{0:T(256)}, u32[]{:S(2)}) copy-start(s32[256]{0:T(256)} %param.11) | copy-start | bytes 3076
  76.7 8.1 %copy-start.1 = (f32[256,60,60]{0,2,1:T(8,128)S(1)}, f32[256,60,60]{0,2,1:T(8,128)}, u32[]{:S(2)}) copy-start(f32[256,60,60]{0,2,1:T(8,128)} %reshape.244) | copy-start | bytes 11059204 | tf_op jit(solution)/shard_map/cond
  162.9 4.7 %copy-start = (f32[3,64,450]{2,1,0:T(8,128)S(1)}, f32[3,64,450]{2,1,0:T(8,128)}, u32[]{:S(2)}) copy-start(f32[3,64,450]{2,1,0:T(8,128)} %param.12) | copy-start | bytes 1036804
  162.9 138.0 %all-to-all-start.1 = ((f32[256,8,450]{0,2,1:T(8,128)}), f32[256,8,450]{0,2,1:T(8,128)}, u32[]{:S(2)}, u32[]{:S(2)}) async-start(f32[256,8,450]{0,2,1:T(8,128)} %all_to_all.33), calls=%async_computation.1 | async-start | bytes 7471104 | tf_op jit(solution)/shard_map/all_to_all | solution.py:107
  167.7 48.2 %collective-permute-start = (f32[3,64,4]{2,1,0:T(8,128)S(1)}, f32[3,64,4]{2,1,0:T(8,128)S(1)}, u32[]{:S(2)}, u32[]{:S(2)}) collective-permute-start(f32[3,64,4]{2,1,0:T(8,128)S(1)} %get-tuple-element.444), channel_id=1, source_target_pairs={{16,0},{32,16},{48,32},{64,48},{80,64},{96,80},{112,96},{0,112},{1... | collective-permute-start | bytes 9224 | tf_op jit(solution)/shard_map/while/body/eval_jaxpr/ppermute | solution.py:24
  173.3 44.7 %collective-permute-start.1 = (f32[3,64,4]{2,1,0:T(8,128)S(1)}, f32[3,64,4]{2,1,0:T(8,128)S(1)}, u32[]{:S(2)}, u32[]{:S(2)}) collective-permute-start(f32[3,64,4]{2,1,0:T(8,128)S(1)} %get-tuple-element.445), channel_id=1, source_target_pairs={{0,16},{16,32},{32,48},{48,64},{64,80},{80,96},{96,112},{112,0},{1... | collective-permute-start | bytes 9224 | tf_op jit(solution)/shard_map/while/body/eval_jaxpr/ppermute | solution.py:23
  218.1 3.0 collective-permute-start.2
  219.5 5.4 %collective-permute-start.3 = (f32[3,4,458]{2,1,0:T(4,128)S(1)}, f32[3,4,458]{2,1,0:T(4,128)S(1)}, u32[]{:S(2)}, u32[]{:S(2)}) collective-permute-start(f32[3,4,458]{2,1,0:T(4,128)S(1)} %get-tuple-element.447), channel_id=1, source_target_pairs={{0,1},{1,2},{2,3},{3,4},{4,5},{5,6},{6,7},{7,8},{8,9},{9,10},{10,1... | collective-permute-start | bytes 65960 | tf_op jit(solution)/shard_map/while/body/eval_jaxpr/ppermute | solution.py:23
  228.3 6.2 %collective-permute-start = (f32[3,64,4]{2,1,0:T(8,128)S(1)}, f32[3,64,4]{2,1,0:T(8,128)S(1)}, u32[]{:S(2)}, u32[]{:S(2)}) collective-permute-start(f32[3,64,4]{2,1,0:T(8,128)S(1)} %get-tuple-element.444), channel_id=1, source_target_pairs={{16,0},{32,16},{48,32},{64,48},{80,64},{96,80},{112,96},{0,112},{1... | collective-permute-start | bytes 9224 | tf_op jit(solution)/shard_map/while/body/eval_jaxpr/ppermute | solution.py:24
  229.6 8.2 %collective-permute-start.1 = (f32[3,64,4]{2,1,0:T(8,128)S(1)}, f32[3,64,4]{2,1,0:T(8,128)S(1)}, u32[]{:S(2)}, u32[]{:S(2)}) collective-permute-start(f32[3,64,4]{2,1,0:T(8,128)S(1)} %get-tuple-element.445), channel_id=1, source_target_pairs={{0,16},{16,32},{32,48},{48,64},{64,80},{80,96},{96,112},{112,0},{1... | collective-permute-start | bytes 9224 | tf_op jit(solution)/shard_map/while/body/eval_jaxpr/ppermute | solution.py:23
  238.0 1.6 collective-permute-start.2
  238.0 5.4 %collective-permute-start.3 = (f32[3,4,458]{2,1,0:T(4,128)S(1)}, f32[3,4,458]{2,1,0:T(4,128)S(1)}, u32[]{:S(2)}, u32[]{:S(2)}) collective-permute-start(f32[3,4,458]{2,1,0:T(4,128)S(1)} %get-tuple-element.447), channel_id=1, source_target_pairs={{0,1},{1,2},{2,3},{3,4},{4,5},{5,6},{6,7},{7,8},{8,9},{9,10},{10,1... | collective-permute-start | bytes 65960 | tf_op jit(solution)/shard_map/while/body/eval_jaxpr/ppermute | solution.py:23
  246.9 6.2 %collective-permute-start = (f32[3,64,4]{2,1,0:T(8,128)S(1)}, f32[3,64,4]{2,1,0:T(8,128)S(1)}, u32[]{:S(2)}, u32[]{:S(2)}) collective-permute-start(f32[3,64,4]{2,1,0:T(8,128)S(1)} %get-tuple-element.444), channel_id=1, source_target_pairs={{16,0},{32,16},{48,32},{64,48},{80,64},{96,80},{112,96},{0,112},{1... | collective-permute-start | bytes 9224 | tf_op jit(solution)/shard_map/while/body/eval_jaxpr/ppermute | solution.py:24
  248.0 8.2 %collective-permute-start.1 = (f32[3,64,4]{2,1,0:T(8,128)S(1)}, f32[3,64,4]{2,1,0:T(8,128)S(1)}, u32[]{:S(2)}, u32[]{:S(2)}) collective-permute-start(f32[3,64,4]{2,1,0:T(8,128)S(1)} %get-tuple-element.445), channel_id=1, source_target_pairs={{0,16},{16,32},{32,48},{48,64},{64,80},{80,96},{96,112},{112,0},{1... | collective-permute-start | bytes 9224 | tf_op jit(solution)/shard_map/while/body/eval_jaxpr/ppermute | solution.py:23
  256.4 1.6 collective-permute-start.2
  256.4 5.4 %collective-permute-start.3 = (f32[3,4,458]{2,1,0:T(4,128)S(1)}, f32[3,4,458]{2,1,0:T(4,128)S(1)}, u32[]{:S(2)}, u32[]{:S(2)}) collective-permute-start(f32[3,4,458]{2,1,0:T(4,128)S(1)} %get-tuple-element.447), channel_id=1, source_target_pairs={{0,1},{1,2},{2,3},{3,4},{4,5},{5,6},{6,7},{7,8},{8,9},{9,10},{10,1... | collective-permute-start | bytes 65960 | tf_op jit(solution)/shard_map/while/body/eval_jaxpr/ppermute | solution.py:23
  265.3 6.2 %collective-permute-start = (f32[3,64,4]{2,1,0:T(8,128)S(1)}, f32[3,64,4]{2,1,0:T(8,128)S(1)}, u32[]{:S(2)}, u32[]{:S(2)}) collective-permute-start(f32[3,64,4]{2,1,0:T(8,128)S(1)} %get-tuple-element.444), channel_id=1, source_target_pairs={{16,0},{32,16},{48,32},{64,48},{80,64},{96,80},{112,96},{0,112},{1... | collective-permute-start | bytes 9224 | tf_op jit(solution)/shard_map/while/body/eval_jaxpr/ppermute | solution.py:24
  265.4 8.3 %collective-permute-start.1 = (f32[3,64,4]{2,1,0:T(8,128)S(1)}, f32[3,64,4]{2,1,0:T(8,128)S(1)}, u32[]{:S(2)}, u32[]{:S(2)}) collective-permute-start(f32[3,64,4]{2,1,0:T(8,128)S(1)} %get-tuple-element.445), channel_id=1, source_target_pairs={{0,16},{16,32},{32,48},{48,64},{64,80},{80,96},{96,112},{112,0},{1... | collective-permute-start | bytes 9224 | tf_op jit(solution)/shard_map/while/body/eval_jaxpr/ppermute | solution.py:23
  273.8 1.6 collective-permute-start.2
  273.9 5.4 %collective-permute-start.3 = (f32[3,4,458]{2,1,0:T(4,128)S(1)}, f32[3,4,458]{2,1,0:T(4,128)S(1)}, u32[]{:S(2)}, u32[]{:S(2)}) collective-permute-start(f32[3,4,458]{2,1,0:T(4,128)S(1)} %get-tuple-element.447), channel_id=1, source_target_pairs={{0,1},{1,2},{2,3},{3,4},{4,5},{5,6},{6,7},{7,8},{8,9},{9,10},{10,1... | collective-permute-start | bytes 65960 | tf_op jit(solution)/shard_map/while/body/eval_jaxpr/ppermute | solution.py:23
  282.7 6.2 %collective-permute-start = (f32[3,64,4]{2,1,0:T(8,128)S(1)}, f32[3,64,4]{2,1,0:T(8,128)S(1)}, u32[]{:S(2)}, u32[]{:S(2)}) collective-permute-start(f32[3,64,4]{2,1,0:T(8,128)S(1)} %get-tuple-element.444), channel_id=1, source_target_pairs={{16,0},{32,16},{48,32},{64,48},{80,64},{96,80},{112,96},{0,112},{1... | collective-permute-start | bytes 9224 | tf_op jit(solution)/shard_map/while/body/eval_jaxpr/ppermute | solution.py:24
  282.8 8.3 %collective-permute-start.1 = (f32[3,64,4]{2,1,0:T(8,128)S(1)}, f32[3,64,4]{2,1,0:T(8,128)S(1)}, u32[]{:S(2)}, u32[]{:S(2)}) collective-permute-start(f32[3,64,4]{2,1,0:T(8,128)S(1)} %get-tuple-element.445), channel_id=1, source_target_pairs={{0,16},{16,32},{32,48},{48,64},{64,80},{80,96},{96,112},{112,0},{1... | collective-permute-start | bytes 9224 | tf_op jit(solution)/shard_map/while/body/eval_jaxpr/ppermute | solution.py:23
  291.2 1.6 collective-permute-start.2
  291.3 5.4 %collective-permute-start.3 = (f32[3,4,458]{2,1,0:T(4,128)S(1)}, f32[3,4,458]{2,1,0:T(4,128)S(1)}, u32[]{:S(2)}, u32[]{:S(2)}) collective-permute-start(f32[3,4,458]{2,1,0:T(4,128)S(1)} %get-tuple-element.447), channel_id=1, source_target_pairs={{0,1},{1,2},{2,3},{3,4},{4,5},{5,6},{6,7},{7,8},{8,9},{9,10},{10,1... | collective-permute-start | bytes 65960 | tf_op jit(solution)/shard_map/while/body/eval_jaxpr/ppermute | solution.py:23
where the time goes:
time: 319 us; the launch traced here: 315 us
  waiting for transfers between devices  133 us (42%)
  matrix products  77 us (24%)
  starting transfers between devices  46.1 us (14%)
  local copies, waits for them, and re-layouts  42.4 us (13%)
  other arithmetic  13.7 us (4%)
    ppermute x12, waiting for transfers between devices, with_halo(): before = lax.ppermute(last, axis, up)  74.5 us
    ppermute x12, waiting for transfers between devices, with_halo(): after = lax.ppermute(initial, axis, down)  58.6 us
    ppermute x12, starting transfers between devices, with_halo(): before = lax.ppermute(last, axis, up)  17.3 us
    ppermute x12, starting transfers between devices, with_halo(): after = lax.ppermute(initial, axis, down)  16 us
    all_to_all x2, local copies, waits for them, and re-layouts, body(): lax.all_to_all(flattened, 'lon', split_axis=0, concat_axis=1, tiled=True)  8.88 us
    all_to_all x1, starting transfers between devices, body(): lax.all_to_all(flattened, 'lon', split_axis=0, concat_axis=1, tiled=True)  8.19 us
    dot_general x1, matrix products, spectral_cut(): step_imag = -jnp.einsum('inb,nm->imb', grid, sin_first, precision=highest)  8.04 us
    dot_general x1, matrix products, spectral_cut(): step_real = jnp.einsum('inb,nm->imb', grid, cos_first, precision=highest)  7.78 us
  transfers between devices with their start and end apart: 26, of which 22 were waited for; matrix products, arithmetic and copies ran while one was open for 6% of the time, Pallas kernels for 0%

commit v1 on v0

v1 whole, which is shorter than its diff:
```python
import functools
import math

import jax
import jax.numpy as jnp
import ml_dtypes
import numpy as np
from jax import lax
from jax.experimental import pallas as pl
from jax.experimental.pallas import tpu as pltpu
from jax.sharding import PartitionSpec as P

MESH = pl.DeviceIdType.MESH
SUB = 20
COEF = 0.65
NLAT = 1024
NLON = 3600
ROWS = 64
COLS = 450
HALF = 32
HALO = 24
TILES = ((0, 128), (128, 256), (256, 384), (384, 450))
ROOT = math.sqrt(0.5)


def fourier_tables():
    k = np.arange(COLS)
    angle = 2.0 * np.pi * (np.outer(k, k) % COLS) / COLS
    both = np.zeros((512, 1024), np.float64)
    both[:COLS, :COLS] = np.cos(angle)
    both[:COLS, 512 : 512 + COLS] = np.sin(angle)
    high = both.astype(ml_dtypes.bfloat16)
    low = (both - high.astype(np.float64)).astype(ml_dtypes.bfloat16)
    twist = np.zeros((8, 512), np.float32)
    for j in range(1, 5):
        twist[2 * (j - 1), :COLS] = np.cos(2.0 * np.pi * j * k / NLON)
        twist[2 * (j - 1) + 1, :COLS] = np.sin(2.0 * np.pi * j * k / NLON)
    return np.stack([high, low]), twist


def place():
    lat = lax.axis_index("lat")
    lon = lax.axis_index("lon")
    ylo = lat // 8
    x = (lat % 8) // 2
    core = lat % 2
    xm = x + ylo * (3 - 2 * x)

    def peer(xm_to, lon_to):
        return {"lat": (ylo * 4 + xm_to + ylo * (3 - 2 * xm_to)) * 2 + core, "lon": lon_to}

    return lat, lon, ylo, core, xm, peer


def split_store(high, low, rows, cols, value):
    top = value.astype(jnp.bfloat16)
    high[rows, cols] = top
    low[rows, cols] = (value - top.astype(jnp.float32)).astype(jnp.bfloat16)


def transform(c, h, base, recv, ybuf, cut_ref, cutb, tw_ref, wv, high, low, acc):
    row_id = lax.broadcasted_iota(jnp.int32, (HALF, 128), 0)
    cuts = jnp.zeros((HALF, 128), jnp.int32)
    for r in range(HALF):
        cuts = jnp.where(row_id == r, cut_ref[base + h * HALF + r], cuts)
    cutb[...] = cuts

    def group(g, rb):
        return pl.ds(g * HALF + rb, 16)

    def product(rows):
        left, small = high[0:rows, :], low[0:rows, :]
        acc[0:rows, :] = (
            jnp.dot(left, wv[0], preferred_element_type=jnp.float32)
            + jnp.dot(small, wv[0], preferred_element_type=jnp.float32)
            + jnp.dot(left, wv[1], preferred_element_type=jnp.float32)
        )

    for rb in (0, 16):
        for lo, hi in TILES:
            cols = pl.ds(lo, hi - lo)
            x = [recv[c, d, pl.ds(rb, 16), cols] for d in range(8)]
            a = [x[d] + x[d + 4] for d in range(4)]
            b = [x[d] - x[d + 4] for d in range(4)]
            diff, total = ROOT * (b[1] - b[3]), ROOT * (b[1] + b[3])
            even, odd = a[0] + a[2], a[1] + a[3]
            real = {1: b[0] + diff, 2: a[0] - a[2], 3: b[0] - diff}
            imag = {1: -total - b[2], 2: a[3] - a[1], 3: b[2] - total}
            split_store(high, low, group(0, rb), cols, even + odd)
            for j in range(1, 5):
                tc = tw_ref[2 * j - 2 : 2 * j - 1, lo:hi]
                ts = tw_ref[2 * j - 1 : 2 * j, lo:hi]
                if j < 4:
                    zr = real[j] * tc + imag[j] * ts
                    zi = imag[j] * tc - real[j] * ts
                else:
                    zr = (even - odd) * tc
                    zi = (odd - even) * ts
                split_store(high, low, group(2 * j - 1, rb), cols, zr)
                split_store(high, low, group(2 * j, rb), cols, zi)
    product(9 * HALF)
    for rb in (0, 16):
        for lo, hi in TILES:
            cols = pl.ds(lo, hi - lo)
            sines = pl.ds(512 + lo, hi - lo)
            limit = cutb[pl.ds(rb, 16), 0 : hi - lo]
            step = 8 * (lax.broadcasted_iota(jnp.int32, (16, hi - lo), 1) + lo)
            for j in range(5):
                wave = step + j
                kept = jnp.minimum(wave, NLON - wave) <= limit
                scale = jnp.where(kept, (2.0 if 0 < j < 4 else 1.0) / NLON, 0.0)
                if j == 0:
                    re = acc[group(0, rb), cols]
                    im = -acc[group(0, rb), sines]
                else:
                    re = acc[group(2 * j - 1, rb), cols] + acc[group(2 * j, rb), sines]
                    im = acc[group(2 * j, rb), cols] - acc[group(2 * j - 1, rb), sines]
                split_store(high, low, group(2 * j, rb), cols, re * scale)
                split_store(high, low, group(2 * j + 1, rb), cols, im * scale)
    product(10 * HALF)
    for rb in (0, 16):
        for lo, hi in TILES:
            cols = pl.ds(lo, hi - lo)
            sines = pl.ds(512 + lo, hi - lo)
            hr, hm = {}, {}
            for j in range(5):
                gr = acc[group(2 * j, rb), cols] - acc[group(2 * j + 1, rb), sines]
                if j == 0:
                    hr[0] = gr
                    continue
                gi = acc[group(2 * j, rb), sines] + acc[group(2 * j + 1, rb), cols]
                tc = tw_ref[2 * j - 2 : 2 * j - 1, lo:hi]
                ts = tw_ref[2 * j - 1 : 2 * j, lo:hi]
                hr[j] = gr * tc - gi * ts
                if j < 4:
                    hm[j] = gr * ts + gi * tc
            even, odd = hr[0] + hr[4], hr[0] - hr[4]
            part = [even + hr[2], odd - hm[2], even - hr[2], odd + hm[2]]
            turn = [
                hr[1] + hr[3],
                ROOT * (hr[1] - hm[1] - hr[3] - hm[3]),
                hm[3] - hm[1],
                ROOT * (hr[3] - hm[3] - hr[1] - hm[1]),
            ]
            for d in range(4):
                ybuf[c, d, pl.ds(rb, 16), cols] = part[d] + turn[d]
                ybuf[c, d + 4, pl.ds(rb, 16), cols] = part[d] - turn[d]


def assemble(store, offset, count, centre, left, right, tail):
    rows = pl.ds(offset, count)
    store[rows, 0:COLS] = centre
    tail[0:count, 0:66] = left
    lane = lax.broadcasted_iota(jnp.int32, (count, 128), 1)
    own = store[rows, 384:512]
    west = pltpu.roll(tail[0:count, :], 62, 1)
    east = pltpu.roll(right, 66, 1)
    store[rows, 384:512] = jnp.where(
        lane < 66, own, jnp.where(lane < 66 + HALO, east, jnp.where(lane >= 128 - HALO, west, 0.0))
    )


def exchange_kernel(
    f_ref, baro_in, land_in, cut_in, w_ref, tw_in,
    filt, flow, opens,
    baro, land, cut_ref, tw_ref, recv, ybuf, crecv, wv, high, low, acc, cutb,
    state, masks, tail,
    lb, lm, rb_, rm, tb, tm, bb, bm, tlb, tlm, trb, trm, blb, blm, brb, brm,
    wsem, hsend, hrecv, rsem, osem, csend, crsem, dsend, fsem,
):
    lat, lon, ylo, core, xm, peer = place()
    lats, lons = 16, 8
    polar = xm == 0
    helper = (xm == 1) | (xm == 3)
    lat_up, lat_down = (lat + 1) % lats, (lat + lats - 1) % lats
    lon_up, lon_down = (lon + 1) % lons, (lon + lons - 1) % lons
    barrier = pltpu.get_barrier_semaphore()

    def greet(device):
        pl.semaphore_signal(barrier, 1, device_id=device, device_id_type=MESH)

    for device in ({"lat": lat_up, "lon": lon}, {"lat": lat_down, "lon": lon}, {"lat": lat, "lon": lon_up}, {"lat": lat, "lon": lon_down}):
        greet(device)

    @pl.when(polar)
    def _():
        for k in range(lons):
            to = (lon + k) % lons
            if k:
                greet(peer(0, to))
            greet(peer(1, to))
            greet(peer(3, to))

    @pl.when(helper)
    def _():
        for k in range(lons):
            to = (lon + k) % lons
            if k:
                greet(peer(xm, to))
            greet(peer(0, to))

    near = [
        pltpu.make_async_copy(baro_in, baro, wsem.at[0]),
        pltpu.make_async_copy(land_in, land, wsem.at[1]),
    ]
    tables = [
        pltpu.make_async_copy(cut_in, cut_ref, wsem.at[2]),
        pltpu.make_async_copy(tw_in, tw_ref, wsem.at[3]),
        pltpu.make_async_copy(w_ref, wv, wsem.at[4]),
    ]
    for copy in near + tables:
        copy.start()
    high[...] = jnp.zeros_like(high)
    low[...] = jnp.zeros_like(low)

    @pl.when(polar)
    def _():
        pl.semaphore_wait(barrier, 27)

    @pl.when(helper)
    def _():
        pl.semaphore_wait(barrier, 19)

    @pl.when(xm == 2)
    def _():
        pl.semaphore_wait(barrier, 4)

    def hop(i, source, target, **to):
        device = {"lat": lat, "lon": lon}
        device.update(to)
        return pltpu.make_async_remote_copy(source, target, hsend.at[i], hrecv.at[i], device_id=device, device_id_type=MESH)

    first = [
        hop(0, baro.at[:, :, pl.ds(384, 66)], lb, lon=lon_up),
        hop(1, land.at[:, pl.ds(384, 66)], lm, lon=lon_up),
        hop(2, baro.at[:, :, pl.ds(0, 128)], rb_, lon=lon_down),
        hop(3, land.at[:, pl.ds(0, 128)], rm, lon=lon_down),
        hop(4, baro.at[:, pl.ds(ROWS - HALO, HALO), :], tb, lat=lat_up),
        hop(5, land.at[pl.ds(ROWS - HALO, HALO), :], tm, lat=lat_up),
        hop(6, baro.at[:, pl.ds(0, HALO), :], bb, lat=lat_down),
        hop(7, land.at[pl.ds(0, HALO), :], bm, lat=lat_down),
    ]
    second = []
    for i, (source, flat, up, upm, down, downm) in enumerate(((lb, lm, tlb, tlm, blb, blm), (rb_, rm, trb, trm, brb, brm))):
        second += [
            hop(8 + 4 * i, source.at[:, pl.ds(ROWS - HALO, HALO), :], up, lat=lat_up),
            hop(9 + 4 * i, flat.at[pl.ds(ROWS - HALO, HALO), :], upm, lat=lat_up),
            hop(10 + 4 * i, source.at[:, pl.ds(0, HALO), :], down, lat=lat_down),
            hop(11 + 4 * i, flat.at[pl.ds(0, HALO), :], downm, lat=lat_down),
        ]
    for copy in near:
        copy.wait()
    for copy in first:
        copy.start()

    @pl.when(polar)
    def _():
        for h in range(2):
            rows = pl.ds(h * HALF, HALF)
            for s in range(2):
                pltpu.make_async_copy(f_ref.at[2 * lon + s, rows, :], recv.at[2 * h + s, lon], rsem.at[2 * h + s]).start()
            for k in range(lons):
                to = (lon + k) % lons

                def send(plane, c, xm_to):
                    pltpu.make_async_remote_copy(
                        f_ref.at[plane, rows, :], recv.at[c, lon], osem, rsem.at[c], device_id=peer(xm_to, to), device_id_type=MESH
                    ).start()

                send(16 + to, 2 * h, 1)
                send(24 + to, 2 * h, 3)
                if k:
                    send(2 * to, 2 * h, 0)
                    send(2 * to + 1, 2 * h + 1, 0)

    for copy in first[:4]:
        copy.wait_recv()
    for copy in second:
        copy.start()
    for copy in first[4:] + second:
        copy.wait_recv()

    for i in range(3):
        assemble(state.at[i], 0, HALO, tb[i], tlb[i], trb[i], tail)
        assemble(state.at[i], HALO, ROWS, baro[i], lb[i], rb_[i], tail)
        assemble(state.at[i], HALO + ROWS, HALO, bb[i], blb[i], brb[i], tail)
    f32 = jnp.float32
    assemble(masks.at[0], 0, HALO, tm[...].astype(f32), tlm[...].astype(f32), trm[...].astype(f32), tail)
    assemble(masks.at[0], HALO, ROWS, land[...].astype(f32), lm[...].astype(f32), rm[...].astype(f32), tail)
    assemble(masks.at[0], HALO + ROWS, HALO, bm[...].astype(f32), blm[...].astype(f32), brm[...].astype(f32), tail)
    total = ROWS + 2 * HALO
    for r in range(0, total, 8):
        rows = pl.ds(r, 8)
        sea = masks[0, rows, :]
        below = masks[0, pl.ds(r + 1, 8), :] if r + 8 < total else sea
        east = sea * pltpu.roll(sea, 511, 1)
        row = (lax.broadcasted_iota(jnp.int32, (8, 512), 0) + (r + NLAT - HALO) + lat * ROWS) % NLAT
        north = jnp.where(row == NLAT - 1, 0.0, sea * below)
        masks[1, rows, :] = east
        masks[2, rows, :] = north
        state[1, rows, :] = state[1, rows, :] * east
        state[2, rows, :] = state[2, rows, :] * north

    def cycle(_, carry):
        for r in range(0, total, 8):
            rows = pl.ds(r, 8)
            e, n = state[1, rows, :], state[2, rows, :]
            above = state[2, pl.ds(r - 1, 8), :] if r else n
            div = e - pltpu.roll(e, 1, 1) + n - above
            state[0, rows, :] = state[0, rows, :] - (COEF * masks[0, rows, :]) * div
        for r in range(0, total, 8):
            rows = pl.ds(r, 8)
            s = state[0, rows, :]
            below = state[0, pl.ds(r + 1, 8), :] if r + 8 < total else s
            state[1, rows, :] = masks[1, rows, :] * (state[1, rows, :] - COEF * (pltpu.roll(s, 511, 1) - s))
            state[2, rows, :] = masks[2, rows, :] * (state[2, rows, :] - COEF * (below - s))
        return carry

    lax.fori_loop(0, SUB, cycle, 0)
    flow[...] = state[:, pl.ds(HALO, ROWS), 0:COLS]
    opens[...] = masks[1:3, pl.ds(HALO, ROWS), 0:COLS]
    for copy in tables:
        copy.wait()

    base = ylo * 128 + core * ROWS
    stride = jnp.where(polar, 1, 2)

    def forward(h):
        pltpu.make_async_copy(crecv.at[0, pl.ds(0, 7)], crecv.at[0, pl.ds(0, 7)], crsem.at[h]).wait()
        rows = pl.ds(pl.multiple_of(h * HALF, HALF), HALF)
        for k in range(lons):
            origin = (lon + k) % lons
            source = crecv.at[h, origin] if k else ybuf.at[2 * h, lon]
            pltpu.make_async_remote_copy(
                source, filt.at[16 + 8 * (xm // 2) + origin, rows, :], dsend, fsem, device_id=peer(0, lon), device_id_type=MESH
            ).start()

    def chunk(i, carry):
        c = i * stride
        h = c // 2
        rows = pl.ds(pl.multiple_of(h * HALF, HALF), HALF)
        pltpu.make_async_copy(recv.at[c], recv.at[c], rsem.at[c]).wait()
        transform(c, h, base, recv, ybuf, cut_ref, cutb, tw_ref, wv, high, low, acc)

        @pl.when(polar)
        def _():
            plane = 2 * lon + c % 2
            pltpu.make_async_copy(ybuf.at[c, lon], filt.at[plane, rows, :], fsem).start()
            for k in range(1, lons):
                to = (lon + k) % lons
                pltpu.make_async_remote_copy(
                    ybuf.at[c, to], filt.at[plane, rows, :], csend, fsem, device_id=peer(0, to), device_id_type=MESH
                ).start()

        @pl.when(helper)
        def _():
            for k in range(1, lons):
                to = (lon + k) % lons
                pltpu.make_async_remote_copy(
                    ybuf.at[c, to], crecv.at[h, lon], csend, crsem.at[h], device_id=peer(xm, to), device_id_type=MESH
                ).start()

            @pl.when(i > 0)
            def _():
                forward(h - 1)

        return carry

    lax.fori_loop(0, jnp.where(polar, 4, jnp.where(helper, 2, 0)), chunk, 0)

    def drain(planes, sem):
        pltpu.make_async_copy(f_ref.at[pl.ds(0, planes)], f_ref.at[pl.ds(0, planes)], sem).wait()

    @pl.when(helper)
    def _():
        forward(1)
        drain(7, csend)
        drain(8, dsend)

    @pl.when(polar)
    def _():
        drain(30, osem)
        drain(14, csend)
        drain(32, fsem)

    for copy in first + second:
        copy.wait_send()


def finish_kernel(thick, f_ref, filt, flow, opens, tracers, velocity, sea, block, made, isem, tsem, vsem):
    lat, lon, ylo, core, xm, peer = place()
    polar = xm == 0
    order = (2, 3, 0, 1)

    def load(source):
        for g in order:
            pltpu.make_async_copy(source.at[pl.ds(8 * g, 8)], block.at[pl.ds(8 * g, 8)], isem.at[g]).start()

    @pl.when(polar)
    def _():
        load(filt)

    @pl.when(jnp.logical_not(polar))
    def _():
        load(f_ref)

    sea[...] = flow[0]
    weight = [thick[k] for k in range(8)]
    whole = functools.reduce(lambda a, b: a + b, weight)
    outs = []
    for c in range(2):
        part = pl.ds(16 + 8 * c, 8)
        pltpu.make_async_copy(f_ref.at[part], block.at[part], isem.at[2 + c]).wait()
        for r in range(0, ROWS, 8):
            rows = pl.ds(r, 8)
            level = [block[16 + 8 * c + k, rows, :] for k in range(8)]
            column = weight[0] * level[0]
            for k in range(1, 8):
                column = column + weight[k] * level[k]
            column = flow[1 + c, rows, :] - column / jnp.full((8, COLS), whole, jnp.float32)
            gate = opens[c, rows, :]
            for k in range(8):
                made[8 * c + k, rows, :] = gate * (level[k] + column)
        outs.append(pltpu.make_async_copy(made.at[pl.ds(8 * c, 8)], velocity.at[pl.ds(8 * c, 8)], vsem.at[c]))
        outs[-1].start()
    for g in range(2):
        part = pl.ds(8 * g, 8)
        pltpu.make_async_copy(f_ref.at[part], block.at[part], isem.at[g]).wait()
        outs.append(pltpu.make_async_copy(block.at[part], tracers.at[part], tsem.at[g]))
        outs[-1].start()
    for copy in outs:
        copy.wait()


def body(fields, thickness, cutoff, barotropic, land_sea):
    f32, i32, bf16 = jnp.float32, jnp.int32, jnp.bfloat16
    planes = fields.reshape(32, ROWS, COLS)
    table, twist = fourier_tables()
    hbm = pl.BlockSpec(memory_space=pltpu.HBM)
    vmem = pl.BlockSpec(memory_space=pltpu.VMEM)
    smem = pl.BlockSpec(memory_space=pltpu.SMEM)
    dma = pltpu.SemaphoreType.DMA
    strips = []
    for rows in (ROWS,):
        strips += [pltpu.VMEM((3, rows, 66), f32), pltpu.VMEM((rows, 66), i32), pltpu.VMEM((3, rows, 128), f32), pltpu.VMEM((rows, 128), i32)]
    strips += [pltpu.VMEM((3, HALO, COLS), f32), pltpu.VMEM((HALO, COLS), i32)] * 2
    strips += [pltpu.VMEM((3, HALO, 66), f32), pltpu.VMEM((HALO, 66), i32), pltpu.VMEM((3, HALO, 128), f32), pltpu.VMEM((HALO, 128), i32)] * 2
    total = ROWS + 2 * HALO
    filt, flow, opens = pl.pallas_call(
        exchange_kernel,
        out_shape=(
            jax.ShapeDtypeStruct((32, ROWS, COLS), f32),
            jax.ShapeDtypeStruct((3, ROWS, COLS), f32),
            jax.ShapeDtypeStruct((2, ROWS, COLS), f32),
        ),
        in_specs=[hbm] * 6,
        out_specs=(hbm, vmem, vmem),
        scratch_shapes=[
            pltpu.VMEM((3, ROWS, COLS), f32),
            pltpu.VMEM((ROWS, COLS), i32),
            pltpu.SMEM((256,), i32),
            pltpu.VMEM((8, 512), f32),
            pltpu.VMEM((4, 8, HALF, COLS), f32),
            pltpu.VMEM((4, 8, HALF, COLS), f32),
            pltpu.VMEM((2, 8, HALF, COLS), f32),
            pltpu.VMEM((2, 512, 1024), bf16),
            pltpu.VMEM((10 * HALF, 512), bf16),
            pltpu.VMEM((10 * HALF, 512), bf16),
            pltpu.VMEM((10 * HALF, 1024), f32),
            pltpu.VMEM((HALF, 128), i32),
            pltpu.VMEM((3, total, 512), f32),
            pltpu.VMEM((3, total, 512), f32),
            pltpu.VMEM((ROWS, 128), f32),
            *strips,
            dma((5,)), dma((16,)), dma((16,)), dma((4,)), dma, dma, dma((2,)), dma, dma,
        ],
        compiler_params=pltpu.CompilerParams(collective_id=1, has_side_effects=True, vmem_limit_bytes=67043328),
    )(planes, barotropic, land_sea, cutoff, jnp.asarray(table), jnp.asarray(twist))
    tracers, velocity, sea = pl.pallas_call(
        finish_kernel,
        out_shape=(
            jax.ShapeDtypeStruct((16, ROWS, COLS), f32),
            jax.ShapeDtypeStruct((16, ROWS, COLS), f32),
            jax.ShapeDtypeStruct((ROWS, COLS), f32),
        ),
        in_specs=[smem, hbm, hbm, vmem, vmem],
        out_specs=(hbm, hbm, vmem),
        scratch_shapes=[pltpu.VMEM((32, ROWS, COLS), f32), pltpu.VMEM((16, ROWS, COLS), f32), dma((4,)), dma((2,)), dma((2,))],
        compiler_params=pltpu.CompilerParams(vmem_limit_bytes=67043328),
    )(thickness, planes, filt, flow, opens)
    shape = (2, 8, ROWS, COLS)
    return tracers.reshape(shape), velocity.reshape(shape), sea


def solution(mesh):
    return jax.shard_map(
        body,
        mesh=mesh,
        in_specs=(P(None, None, "lat", "lon"), P(), P(), P(None, "lat", "lon"), P("lat", "lon")),
        out_specs=(P(None, None, "lat", "lon"), P(None, None, "lat", "lon"), P("lat", "lon")),
        check_vma=False,
    )
```

time: 319 us -> 76.1 us (0.24)
  the two profiles are of different devices: /device:TPU:0 before, /device:TPU:1 now
where the time goes in v1:
time: 76.1 us; the launch traced here: 76 us
  Pallas kernels  75.3 us (99%)
    pallas_call x1, Pallas kernels, body(): pl.pallas_call(exchange_kernel, out_shape=(jax.ShapeDtypeStruct((32, ROWS...  70.1 us
    pallas_call x1, Pallas kernels, body(): pl.pallas_call(finish_kernel, out_shape=(jax.ShapeDtypeStruct((16, ROWS,...  5.21 us

profile of v1, /device:TPU:1, one launch (start us, length us, event | category | flops | bytes accessed | tf_op | source)
XLA Modules:
  0.0 76.0 jit_solution(10662925319085271548)
XLA Ops:
  0.6 70.1 %shard_map.94 = (f32[32,64,450]{2,1,0:T(8,128)}, f32[3,64,450]{2,1,0:T(8,128)}, f32[2,64,450]{2,1,0:T(8,128)}) custom-call(f32[32,64,450]{2,1,0:T(8,128)} %bitcast.3, f32[3,64,450]{2,1,0:T(8,128)} %baro_in.1, s32[64,450]{1,0:T(8,128)} %land_in.1, s32[256]{0:T(256)} %cut_in.1, bf16[2,512,1024]{2,1,0:T(8,128)(2,1)} %constant.4.clone.w_ref, ...), custom_call_target="tpu_custom_call" | custom-call | tf_op jit(solution)/shard_map/pallas_call | solution.py:449
  70.7 5.2 %shard_map.95 = (f32[16,64,450]{2,1,0:T(8,128)}, f32[16,64,450]{2,1,0:T(8,128)}, f32[64,450]{1,0:T(8,128)}) custom-call(f32[8]{0:T(128)} %thick.1, f32[32,64,450]{2,1,0:T(8,128)} %bitcast.4, f32[32,64,450]{2,1,0:T(8,128)} %get-tuple-element.9.filt, f32[3,64,450]{2,1,0:T(8,128)} %get-tuple-element.10.flow, f32[2,64,450]{2,1,0:T(8,128)} %get-tuple-element.11.opens), custom_call_target="tpu_custom_call" | custom-call | tf_op jit(solution)/shard_map/pallas_call | solution.py:479

commit v2 on v1

v2 whole, which is shorter than its diff:
```python
import functools
import math

import jax
import jax.numpy as jnp
import ml_dtypes
import numpy as np
from jax import lax
from jax.experimental import pallas as pl
from jax.experimental.pallas import tpu as pltpu
from jax.sharding import PartitionSpec as P

MESH = pl.DeviceIdType.MESH
SUB = 20
COEF = 0.65
NLAT = 1024
NLON = 3600
ROWS = 64
COLS = 450
PART = 8
EACH = ROWS // PART
TAKES = (14, 9, 0, 9)
STARTS = (0, 112, 184, 184)
LAG = 2
AHEAD = 4
HALO = 24
TILES = ((0, 128), (128, 256), (256, 384), (384, 450))
ROOT = math.sqrt(0.5)


def fourier_tables():
    k = np.arange(COLS)
    angle = 2.0 * np.pi * (np.outer(k, k) % COLS) / COLS
    both = np.zeros((512, 1024), np.float64)
    both[:COLS, :COLS] = np.cos(angle)
    both[:COLS, 512 : 512 + COLS] = np.sin(angle)
    high = both.astype(ml_dtypes.bfloat16)
    low = (both - high.astype(np.float64)).astype(ml_dtypes.bfloat16)
    twist = np.zeros((8, 512), np.float32)
    for j in range(1, 5):
        twist[2 * (j - 1), :COLS] = np.cos(2.0 * np.pi * j * k / NLON)
        twist[2 * (j - 1) + 1, :COLS] = np.sin(2.0 * np.pi * j * k / NLON)
    return np.stack([high, low]), twist


def place():
    lat = lax.axis_index("lat")
    lon = lax.axis_index("lon")
    ylo = lat // 8
    x = (lat % 8) // 2
    core = lat % 2
    xm = x + ylo * (3 - 2 * x)

    def peer(xm_to, lon_to):
        return {"lat": (ylo * 4 + xm_to + ylo * (3 - 2 * xm_to)) * 2 + core, "lon": lon_to}

    return lat, lon, ylo, core, xm, peer


def split_store(terms, j, cols, real, imag):
    value = jnp.concatenate([real, imag], axis=0)
    top = value.astype(jnp.bfloat16)
    terms[pl.ds(2 * PART * j, 2 * PART), cols] = top
    terms[pl.ds(10 * PART + 2 * PART * j, 2 * PART), cols] = (value - top.astype(jnp.float32)).astype(jnp.bfloat16)


def transform(c, base, recv, ybuf, cut_ref, cutb, tw_ref, wv, terms, acc):
    row_id = lax.broadcasted_iota(jnp.int32, (PART, 128), 0)
    cuts = jnp.zeros((PART, 128), jnp.int32)
    for r in range(PART):
        cuts = jnp.where(row_id == r, cut_ref[base + r], cuts)
    cutb[...] = cuts

    def product():
        both = jnp.dot(terms[...], wv[0], preferred_element_type=jnp.float32)
        fine = jnp.dot(terms[0 : 10 * PART, :], wv[1], preferred_element_type=jnp.float32)
        acc[...] = both[0 : 10 * PART] + both[10 * PART :] + fine

    def part(j, imag, cols):
        return acc[pl.ds(2 * PART * j + PART * imag, PART), cols]

    for lo, hi in TILES:
        cols = pl.ds(lo, hi - lo)
        x = [recv[c, d, :, cols] for d in range(8)]
        a = [x[d] + x[d + 4] for d in range(4)]
        b = [x[d] - x[d + 4] for d in range(4)]
        diff, total = ROOT * (b[1] - b[3]), ROOT * (b[1] + b[3])
        even, odd = a[0] + a[2], a[1] + a[3]
        real = {1: b[0] + diff, 2: a[0] - a[2], 3: b[0] - diff}
        imag = {1: -total - b[2], 2: a[3] - a[1], 3: b[2] - total}
        split_store(terms, 0, cols, even + odd, jnp.zeros_like(even))
        for j in range(1, 5):
            tc = tw_ref[2 * j - 2 : 2 * j - 1, lo:hi]
            ts = tw_ref[2 * j - 1 : 2 * j, lo:hi]
            if j < 4:
                split_store(terms, j, cols, real[j] * tc + imag[j] * ts, imag[j] * tc - real[j] * ts)
            else:
                split_store(terms, j, cols, (even - odd) * tc, (odd - even) * ts)
    product()
    for lo, hi in TILES:
        cols = pl.ds(lo, hi - lo)
        sines = pl.ds(512 + lo, hi - lo)
        limit = cutb[:, 0 : hi - lo]
        step = 8 * (lax.broadcasted_iota(jnp.int32, (PART, hi - lo), 1) + lo)
        for j in range(5):
            wave = step + j
            kept = jnp.minimum(wave, NLON - wave) <= limit
            scale = jnp.where(kept, (2.0 if 0 < j < 4 else 1.0) / NLON, 0.0)
            re = part(j, 0, cols) + part(j, 1, sines)
            im = part(j, 1, cols) - part(j, 0, sines)
            split_store(terms, j, cols, re * scale, im * scale)
    product()
    for lo, hi in TILES:
        cols = pl.ds(lo, hi - lo)
        sines = pl.ds(512 + lo, hi - lo)
        hr, hm = {}, {}
        for j in range(5):
            gr = part(j, 0, cols) - part(j, 1, sines)
            if j == 0:
                hr[0] = gr
                continue
            gi = part(j, 0, sines) + part(j, 1, cols)
            tc = tw_ref[2 * j - 2 : 2 * j - 1, lo:hi]
            ts = tw_ref[2 * j - 1 : 2 * j, lo:hi]
            hr[j] = gr * tc - gi * ts
            if j < 4:
                hm[j] = gr * ts + gi * tc
        even, odd = hr[0] + hr[4], hr[0] - hr[4]
        plain = [even + hr[2], odd - hm[2], even - hr[2], odd + hm[2]]
        turn = [
            hr[1] + hr[3],
            ROOT * (hr[1] - hm[1] - hr[3] - hm[3]),
            hm[3] - hm[1],
            ROOT * (hr[3] - hm[3] - hr[1] - hm[1]),
        ]
        for d in range(4):
            ybuf[c, d, :, cols] = plain[d] + turn[d]
            ybuf[c, d + 4, :, cols] = plain[d] - turn[d]


def assemble(store, offset, count, centre, left, right, tail):
    rows = pl.ds(offset, count)
    store[rows, 0:COLS] = centre
    tail[0:count, 0:66] = left
    lane = lax.broadcasted_iota(jnp.int32, (count, 128), 1)
    own = store[rows, 384:512]
    west = pltpu.roll(tail[0:count, :], 62, 1)
    east = pltpu.roll(right, 66, 1)
    store[rows, 384:512] = jnp.where(
        lane < 66, own, jnp.where(lane < 66 + HALO, east, jnp.where(lane >= 128 - HALO, west, 0.0))
    )


def exchange_kernel(
    f_ref, baro_in, land_in, cut_in, w_ref, tw_in,
    filt, flow, opens,
    baro, land, cut_ref, tw_ref, recv, ybuf, crecv, wv, terms, acc, cutb,
    state, masks, tail, held_flow, held_opens,
    lb, lm, rb_, rm, tb, tm, bb, bm, tlb, tlm, trb, trm, blb, blm, brb, brm,
    wsem, hsend, hrecv, rsem, osem, csend, crsem, dsend, fsem,
):
    lat, lon, ylo, core, xm, peer = place()
    lats, lons = 16, 8
    polar = xm == 0
    helper = (xm == 1) | (xm == 3)
    lat_up, lat_down = (lat + 1) % lats, (lat + lats - 1) % lats
    lon_up, lon_down = (lon + 1) % lons, (lon + lons - 1) % lons
    barrier = pltpu.get_barrier_semaphore()

    def greet(device):
        pl.semaphore_signal(barrier, 1, device_id=device, device_id_type=MESH)

    for lat_to in (lat, lat_up, lat_down):
        for lon_to in (lon, lon_up, lon_down):
            if lat_to is not lat or lon_to is not lon:
                greet({"lat": lat_to, "lon": lon_to})

    @pl.when(polar)
    def _():
        for k in range(lons):
            to = (lon + k) % lons
            if k:
                greet(peer(0, to))
            greet(peer(1, to))
            greet(peer(3, to))

    @pl.when(helper)
    def _():
        for k in range(lons):
            to = (lon + k) % lons
            if k:
                greet(peer(xm, to))
            greet(peer(0, to))

    near = [
        pltpu.make_async_copy(baro_in, baro, wsem.at[0]),
        pltpu.make_async_copy(land_in, land, wsem.at[1]),
    ]
    tables = [
        pltpu.make_async_copy(cut_in, cut_ref, wsem.at[2]),
        pltpu.make_async_copy(tw_in, tw_ref, wsem.at[3]),
        pltpu.make_async_copy(w_ref, wv, wsem.at[4]),
    ]
    for copy in near + tables:
        copy.start()
    terms[...] = jnp.zeros_like(terms)

    @pl.when(polar)
    def _():
        pl.semaphore_wait(barrier, 31)

    @pl.when(helper)
    def _():
        pl.semaphore_wait(barrier, 23)

    @pl.when(xm == 2)
    def _():
        pl.semaphore_wait(barrier, 8)

    def hop(i, source, target, **to):
        device = {"lat": lat, "lon": lon}
        device.update(to)
        return pltpu.make_async_remote_copy(source, target, hsend.at[i], hrecv.at[i], device_id=device, device_id_type=MESH)

    first = [
        hop(0, baro.at[:, :, pl.ds(384, 66)], lb, lon=lon_up),
        hop(1, land.at[:, pl.ds(384, 66)], lm, lon=lon_up),
        hop(2, baro.at[:, :, pl.ds(0, 128)], rb_, lon=lon_down),
        hop(3, land.at[:, pl.ds(0, 128)], rm, lon=lon_down),
        hop(4, baro.at[:, pl.ds(ROWS - HALO, HALO), :], tb, lat=lat_up),
        hop(5, land.at[pl.ds(ROWS - HALO, HALO), :], tm, lat=lat_up),
        hop(6, baro.at[:, pl.ds(0, HALO), :], bb, lat=lat_down),
        hop(7, land.at[pl.ds(0, HALO), :], bm, lat=lat_down),
    ]
    low_rows, top_rows = pl.ds(ROWS - HALO, HALO), pl.ds(0, HALO)
    west_cols, east_cols = pl.ds(384, 66), pl.ds(0, 128)
    corners = ((low_rows, lat_up, tlb, tlm, trb, trm), (top_rows, lat_down, blb, blm, brb, brm))
    for i, (part, lat_to, left, leftm, right, rightm) in enumerate(corners):
        first += [
            hop(8 + 4 * i, baro.at[:, part, west_cols], left, lat=lat_to, lon=lon_up),
            hop(9 + 4 * i, land.at[part, west_cols], leftm, lat=lat_to, lon=lon_up),
            hop(10 + 4 * i, baro.at[:, part, east_cols], right, lat=lat_to, lon=lon_down),
            hop(11 + 4 * i, land.at[part, east_cols], rightm, lat=lat_to, lon=lon_down),
        ]
    for copy in near:
        copy.wait()
    for copy in first:
        copy.start()

    def chunk_of(xm_of, lon_of, i):
        unit = STARTS[xm_of] + lon_of * TAKES[xm_of] + i
        return unit // EACH, pl.ds(pl.multiple_of(unit % EACH * PART, PART), PART)

    def drain(chunks, sem):
        if chunks // EACH:
            whole = f_ref.at[pl.ds(0, chunks // EACH)]
            pltpu.make_async_copy(whole, whole, sem).wait()
        if chunks % EACH:
            rest = f_ref.at[0, pl.ds(0, chunks % EACH * PART), :]
            pltpu.make_async_copy(rest, rest, sem).wait()

    def settle(i):
        drain(7 + 16 * (i < TAKES[1]), osem.at[i])

    def deal(i):
        plane, rows = chunk_of(0, lon, i)
        pltpu.make_async_copy(f_ref.at[plane, rows, :], recv.at[i, lon], rsem.at[i]).start()

        def one(k, carry):
            to = (lon + k) % lons

            def send(xm_to):
                plane, rows = chunk_of(xm_to, to, i)
                pltpu.make_async_remote_copy(
                    f_ref.at[plane, rows, :], recv.at[i, lon], osem.at[i], rsem.at[i], device_id=peer(xm_to, to), device_id_type=MESH
                ).start()

            if i < TAKES[1]:
                send(1)
                send(3)

            @pl.when(k > 0)
            def _():
                send(0)

            return carry

        lax.fori_loop(0, lons, one, 0)

    @pl.when(polar)
    def _():
        for i in range(AHEAD):
            deal(i)

    for copy in first:
        copy.wait_recv()

    for i in range(3):
        assemble(state.at[i], 0, HALO, tb[i], tlb[i], trb[i], tail)
        assemble(state.at[i], HALO, ROWS, baro[i], lb[i], rb_[i], tail)
        assemble(state.at[i], HALO + ROWS, HALO, bb[i], blb[i], brb[i], tail)
    f32 = jnp.float32
    assemble(masks.at[0], 0, HALO, tm[...].astype(f32), tlm[...].astype(f32), trm[...].astype(f32), tail)
    assemble(masks.at[0], HALO, ROWS, land[...].astype(f32), lm[...].astype(f32), rm[...].astype(f32), tail)
    assemble(masks.at[0], HALO + ROWS, HALO, bm[...].astype(f32), blm[...].astype(f32), brm[...].astype(f32), tail)
    total = ROWS + 2 * HALO
    for r in range(0, total, 8):
        rows = pl.ds(r, 8)
        sea = masks[0, rows, :]
        below = masks[0, pl.ds(r + 1, 8), :] if r + 8 < total else sea
        east = sea * pltpu.roll(sea, 511, 1)
        row = (lax.broadcasted_iota(jnp.int32, (8, 512), 0) + (r + NLAT - HALO) + lat * ROWS) % NLAT
        north = jnp.where(row == NLAT - 1, 0.0, sea * below)
        masks[1, rows, :] = east
        masks[2, rows, :] = north
        state[1, rows, :] = state[1, rows, :] * east
        state[2, rows, :] = state[2, rows, :] * north

    def cycle(_, carry):
        for r in range(0, total, 8):
            rows = pl.ds(r, 8)
            e, n = state[1, rows, :], state[2, rows, :]
            above = state[2, pl.ds(r - 1, 8), :] if r else n
            div = e - pltpu.roll(e, 1, 1) + n - above
            state[0, rows, :] = state[0, rows, :] - (COEF * masks[0, rows, :]) * div
        for r in range(0, total, 8):
            rows = pl.ds(r, 8)
            s = state[0, rows, :]
            below = state[0, pl.ds(r + 1, 8), :] if r + 8 < total else s
            state[1, rows, :] = masks[1, rows, :] * (state[1, rows, :] - COEF * (pltpu.roll(s, 511, 1) - s))
            state[2, rows, :] = masks[2, rows, :] * (state[2, rows, :] - COEF * (below - s))
        return carry

    for copy in tables:
        copy.wait()

    base = ylo * 128 + core * ROWS
    far = xm // 2
    start = STARTS[1] + (STARTS[3] - STARTS[1]) * far

    def forward(i):
        pltpu.make_async_copy(crecv.at[0, pl.ds(0, 7)], crecv.at[0, pl.ds(0, 7)], crsem.at[i]).wait()

        def to_polar(source, origin):
            unit = start + origin * TAKES[1] + i
            rows = pl.ds(pl.multiple_of(unit % EACH * PART, PART), PART)
            pltpu.make_async_remote_copy(
                source, filt.at[unit // EACH, rows, :], dsend, fsem, device_id=peer(0, lon), device_id_type=MESH
            ).start()

        to_polar(ybuf.at[i, lon], lon)

        def relay(k, carry):
            origin = (lon + k) % lons
            to_polar(crecv.at[i, origin], origin)
            return carry

        lax.fori_loop(1, lons, relay, 0)

    @pl.when(polar)
    def _():
        for i in range(2):
            settle(i)
            deal(i + AHEAD)

    def chunk(i, carry):
        unit = jnp.where(polar, lon * TAKES[0], start + lon * TAKES[1]) + i
        plane = unit // EACH
        row = pl.multiple_of(unit % EACH * PART, PART)

        @pl.when(polar | helper)
        def _():
            pltpu.make_async_copy(recv.at[i], recv.at[i], rsem.at[i]).wait()
            transform(i, base + row, recv, ybuf, cut_ref, cutb, tw_ref, wv, terms, acc)

        @pl.when(polar)
        def _():
            target = filt.at[plane, pl.ds(row, PART), :]
            pltpu.make_async_copy(ybuf.at[i, lon], target, fsem).start()

            def back(k, carry):
                to = (lon + k) % lons
                pltpu.make_async_remote_copy(ybuf.at[i, to], target, csend, fsem, device_id=peer(0, to), device_id_type=MESH).start()
                return carry

            lax.fori_loop(1, lons, back, 0)
            for g in range(TAKES[0] - AHEAD - 2):

                @pl.when(i == g)
                def _():
                    settle(g + 2)
                    deal(g + 2 + AHEAD)

        @pl.when(helper)
        def _():
            def swap(k, carry):
                to = (lon + k) % lons
                pltpu.make_async_remote_copy(
                    ybuf.at[i, to], crecv.at[i, lon], csend, crsem.at[i], device_id=peer(xm, to), device_id_type=MESH
                ).start()
                return carry

            lax.fori_loop(1, lons, swap, 0)

        lax.fori_loop(0, jnp.where(i < TAKES[1], SUB // TAKES[1], 0) + jnp.where(i < SUB % TAKES[1], 1, 0), cycle, 0)

        @pl.when(helper & (i >= LAG))
        def _():
            forward(i - LAG)

        return carry

    lax.fori_loop(0, jnp.where(polar, TAKES[0], TAKES[1]), chunk, 0)
    held_flow[...] = state[:, pl.ds(HALO, ROWS), 0:COLS]
    held_opens[...] = masks[1:3, pl.ds(HALO, ROWS), 0:COLS]
    made = [pltpu.make_async_copy(held_flow, flow, wsem.at[0]), pltpu.make_async_copy(held_opens, opens, wsem.at[1])]
    for copy in made:
        copy.start()

    @pl.when(helper)
    def _():
        for i in range(TAKES[1] - LAG, TAKES[1]):
            forward(i)
        drain(7 * TAKES[1], csend)
        drain(8 * TAKES[1], dsend)

    @pl.when(polar)
    def _():
        for i in range(TAKES[0] - AHEAD, TAKES[0]):
            settle(i)
        drain(7 * TAKES[0], csend)
        drain(32 * EACH, fsem)

    for copy in made:
        copy.wait()
    for copy in first:
        copy.wait_send()


def finish_kernel(thick_in, f_ref, filt, flow_in, opens_in, tracers, velocity, sea, thick, flow, opens, block, made, isem, tsem, vsem, wsem):
    lat, lon, ylo, core, xm, peer = place()
    polar = xm == 0
    pieces = [(q, g) for q in range(4) for g in (2, 3, 0, 1)]

    def view(ref, q, g):
        return ref.at[pl.ds(8 * g, 8), pl.ds(16 * q, 16), :]

    def load(source):
        for q, g in pieces:
            pltpu.make_async_copy(view(source, q, g), view(block, q, g), isem.at[q, g]).start()

    @pl.when(polar)
    def _():
        load(filt)

    @pl.when(jnp.logical_not(polar))
    def _():
        load(f_ref)

    small = [pltpu.make_async_copy(flow_in, flow, wsem.at[0]), pltpu.make_async_copy(opens_in, opens, wsem.at[1]), pltpu.make_async_copy(thick_in, thick, wsem.at[3])]
    for copy in small:
        copy.start()
    for copy in small:
        copy.wait()
    weight = [thick[k] for k in range(8)]
    whole = functools.reduce(lambda a, b: a + b, weight)
    share = 1.0 / jnp.full((8, COLS), whole, jnp.float32)
    outs = [pltpu.make_async_copy(flow.at[0], sea, wsem.at[2])]
    outs[0].start()
    for q, g in pieces:
        pltpu.make_async_copy(view(f_ref, q, g), view(block, q, g), isem.at[q, g]).wait()
        if g < 2:
            outs.append(pltpu.make_async_copy(view(block, q, g), view(tracers, q, g), tsem.at[q, g]))
        else:
            c = g - 2
            for r in range(16 * q, 16 * q + 16, 8):
                rows = pl.ds(r, 8)
                level = [block[8 * g + k, rows, :] for k in range(8)]
                column = weight[0] * level[0]
                for k in range(1, 8):
                    column = column + weight[k] * level[k]
                column = flow[1 + c, rows, :] - column * share
                gate = opens[c, rows, :]
                for k in range(8):
                    made[8 * c + k, rows, :] = gate * (level[k] + column)
            outs.append(pltpu.make_async_copy(view(made, q, c), view(velocity, q, c), vsem.at[q, c]))
        outs[-1].start()
    for copy in outs:
        copy.wait()


def body(fields, thickness, cutoff, barotropic, land_sea):
    f32, i32, bf16 = jnp.float32, jnp.int32, jnp.bfloat16
    planes = fields.reshape(32, ROWS, COLS)
    table, twist = fourier_tables()
    hbm = pl.BlockSpec(memory_space=pltpu.HBM)
    dma = pltpu.SemaphoreType.DMA
    strips = []
    for rows in (ROWS,):
        strips += [pltpu.VMEM((3, rows, 66), f32), pltpu.VMEM((rows, 66), i32), pltpu.VMEM((3, rows, 128), f32), pltpu.VMEM((rows, 128), i32)]
    strips += [pltpu.VMEM((3, HALO, COLS), f32), pltpu.VMEM((HALO, COLS), i32)] * 2
    strips += [pltpu.VMEM((3, HALO, 66), f32), pltpu.VMEM((HALO, 66), i32), pltpu.VMEM((3, HALO, 128), f32), pltpu.VMEM((HALO, 128), i32)] * 2
    total = ROWS + 2 * HALO
    filt, flow, opens = pl.pallas_call(
        exchange_kernel,
        out_shape=(
            jax.ShapeDtypeStruct((32, ROWS, COLS), f32),
            jax.ShapeDtypeStruct((3, ROWS, COLS), f32),
            jax.ShapeDtypeStruct((2, ROWS, COLS), f32),
        ),
        in_specs=[hbm] * 6,
        out_specs=(hbm, hbm, hbm),
        scratch_shapes=[
            pltpu.VMEM((3, ROWS, COLS), f32),
            pltpu.VMEM((ROWS, COLS), i32),
            pltpu.SMEM((256,), i32),
            pltpu.VMEM((8, 512), f32),
            pltpu.VMEM((TAKES[0], 8, PART, COLS), f32),
            pltpu.VMEM((TAKES[0], 8, PART, COLS), f32),
            pltpu.VMEM((TAKES[1], 8, PART, COLS), f32),
            pltpu.VMEM((2, 512, 1024), bf16),
            pltpu.VMEM((20 * PART, 512), bf16),
            pltpu.VMEM((10 * PART, 1024), f32),
            pltpu.VMEM((PART, 128), i32),
            pltpu.VMEM((3, total, 512), f32),
            pltpu.VMEM((3, total, 512), f32),
            pltpu.VMEM((ROWS, 128), f32),
            pltpu.VMEM((3, ROWS, COLS), f32),
            pltpu.VMEM((2, ROWS, COLS), f32),
            *strips,
            dma((5,)), dma((16,)), dma((16,)), dma((TAKES[0],)), dma((TAKES[0],)), dma, dma((TAKES[1],)), dma, dma,
        ],
        compiler_params=pltpu.CompilerParams(collective_id=1, has_side_effects=True, vmem_limit_bytes=67043328),
    )(planes, barotropic, land_sea, cutoff, jnp.asarray(table), jnp.asarray(twist))
    tracers, velocity, sea = pl.pallas_call(
        finish_kernel,
        out_shape=(
            jax.ShapeDtypeStruct((16, ROWS, COLS), f32),
            jax.ShapeDtypeStruct((16, ROWS, COLS), f32),
            jax.ShapeDtypeStruct((ROWS, COLS), f32),
        ),
        in_specs=[hbm] * 5,
        out_specs=(hbm, hbm, hbm),
        scratch_shapes=[pltpu.SMEM((8,), f32), pltpu.VMEM((3, ROWS, COLS), f32), pltpu.VMEM((2, ROWS, COLS), f32), pltpu.VMEM((32, ROWS, COLS), f32), pltpu.VMEM((16, ROWS, COLS), f32), dma((4, 4)), dma((4, 2)), dma((4, 2)), dma((4,))],
        compiler_params=pltpu.CompilerParams(vmem_limit_bytes=67043328),
    )(thickness, planes, filt, flow, opens)
    shape = (2, 8, ROWS, COLS)
    return tracers.reshape(shape), velocity.reshape(shape), sea


def solution(mesh):
    return jax.shard_map(
        body,
        mesh=mesh,
        in_specs=(P(None, None, "lat", "lon"), P(), P(), P(None, "lat", "lon"), P("lat", "lon")),
        out_specs=(P(None, None, "lat", "lon"), P(None, None, "lat", "lon"), P("lat", "lon")),
        check_vma=False,
    )
```

time: 76.1 us -> 69.2 us (0.909)
  Pallas kernels: 75.3 us -> 68.5 us
    pallas_call x1, Pallas kernels: 70.1 us -> 63.8 us  [body(): pl.pallas_call(exchange_kernel, out_shape=(jax.ShapeDtypeStruct((32, ROWS...]
where the time goes in v2:
time: 69.2 us; the launch traced here: 69.1 us
  Pallas kernels  68.5 us (99%)
    pallas_call x1, Pallas kernels, body(): pl.pallas_call(exchange_kernel, out_shape=(jax.ShapeDtypeStruct((32, ROWS...  63.8 us
    pallas_call x1, Pallas kernels, body(): pl.pallas_call(finish_kernel, out_shape=(jax.ShapeDtypeStruct((16, ROWS,...  4.74 us

profile of v2, /device:TPU:1, one launch (start us, length us, event | category | flops | bytes accessed | tf_op | source)
XLA Modules:
  0.0 69.1 jit_solution(12878791932643007117)
XLA Ops:
  0.6 63.8 %shard_map.94 = (f32[32,64,450]{2,1,0:T(8,128)}, f32[3,64,450]{2,1,0:T(8,128)}, f32[2,64,450]{2,1,0:T(8,128)}) custom-call(f32[32,64,450]{2,1,0:T(8,128)} %bitcast.3, f32[3,64,450]{2,1,0:T(8,128)} %baro_in.1, s32[64,450]{1,0:T(8,128)} %land_in.1, s32[256]{0:T(256)} %cut_in.1, bf16[2,512,1024]{2,1,0:T(8,128)(2,1)} %constant.4.clone.w_ref, ...), custom_call_target="tpu_custom_call" | custom-call | tf_op jit(solution)/shard_map/pallas_call | solution.py:504
  64.4 4.7 %shard_map.95 = (f32[16,64,450]{2,1,0:T(8,128)}, f32[16,64,450]{2,1,0:T(8,128)}, f32[64,450]{1,0:T(8,128)}) custom-call(f32[8]{0:T(128)} %thick_in.1, f32[32,64,450]{2,1,0:T(8,128)} %bitcast.4, f32[32,64,450]{2,1,0:T(8,128)} %get-tuple-element.9.filt, f32[3,64,450]{2,1,0:T(8,128)} %get-tuple-element.10.flow_in, f32[2,64,450]{2,1,0:T(8,128)} %get-tuple-element.11.opens_in), custom_call_target="tpu_custom_call" | custom-call | tf_op jit(solution)/shard_map/pallas_call | solution.py:535

commit v3 on v2

--- a/solution.py
+++ b/solution.py
@@ -19,10 +19,10 @@
 COLS = 450
 PART = 8
 EACH = ROWS // PART
-TAKES = (14, 9, 0, 9)
-STARTS = (0, 112, 184, 184)
+TAKES = (13, 10, 0, 9)
+STARTS = (0, 104, 184, 184)
 LAG = 2
-AHEAD = 4
+AHEAD = 6
 HALO = 24
 TILES = ((0, 128), (128, 256), (256, 384), (384, 450))
 ROOT = math.sqrt(0.5)
@@ -244,8 +244,11 @@
         ]
     for copy in near:
         copy.wait()
-    for copy in first:
-        copy.start()
+
+    @pl.when(jnp.logical_not(polar))
+    def _():
+        for copy in first:
+            copy.start()
 
     def chunk_of(xm_of, lon_of, i):
         unit = STARTS[xm_of] + lon_of * TAKES[xm_of] + i
@@ -259,38 +262,120 @@
             rest = f_ref.at[0, pl.ds(0, chunks % EACH * PART), :]
             pltpu.make_async_copy(rest, rest, sem).wait()
 
-    def settle(i):
-        drain(7 + 16 * (i < TAKES[1]), osem.at[i])
-
-    def deal(i):
+    def send(i, xm_to, lon_to):
+        plane, rows = chunk_of(xm_to, lon_to, i)
+        pltpu.make_async_remote_copy(
+            f_ref.at[plane, rows, :], recv.at[i, lon], osem, rsem.at[i], device_id=peer(xm_to, lon_to), device_id_type=MESH
+        ).start()
+
+    def deal_near(i):
         plane, rows = chunk_of(0, lon, i)
         pltpu.make_async_copy(f_ref.at[plane, rows, :], recv.at[i, lon], rsem.at[i]).start()
 
         def one(k, carry):
+            send(i, 0, (lon + k) % lons)
+            return carry
+
+        lax.fori_loop(1, lons, one, 0)
+
+    def deal_far(i, carry):
+        def one(k, carry):
             to = (lon + k) % lons
-
-            def send(xm_to):
-                plane, rows = chunk_of(xm_to, to, i)
+            send(i, 1, to)
+
+            @pl.when(i < TAKES[3])
+            def _():
+                send(i, 3, to)
+
+            return carry
+
+        return lax.fori_loop(0, lons, one, carry)
+
+    @pl.when(polar)
+    def _():
+        deal_far(0, 0)
+        for i in range(AHEAD):
+            deal_near(i)
+        lax.fori_loop(1, TAKES[1], deal_far, 0)
+        for copy in first:
+            copy.start()
+
+    for copy in tables:
+        copy.wait()
+
+    base = ylo * 128 + core * ROWS
+    far = xm // 2
+    mine = jnp.where(polar, TAKES[0], jnp.where(helper, TAKES[1] + far * (TAKES[3] - TAKES[1]), 0))
+    start = STARTS[1] + (STARTS[3] - STARTS[1]) * far
+
+    def forward(i):
+        pltpu.make_async_copy(crecv.at[0, pl.ds(0, 7)], crecv.at[0, pl.ds(0, 7)], crsem.at[i]).wait()
+
+        def to_polar(source, origin):
+            unit = start + origin * mine + i
+            rows = pl.ds(pl.multiple_of(unit % EACH * PART, PART), PART)
+            pltpu.make_async_remote_copy(
+                source, filt.at[unit // EACH, rows, :], dsend, fsem, device_id=peer(0, lon), device_id_type=MESH
+            ).start()
+
+        to_polar(ybuf.at[i, lon], lon)
+
+        def relay(k, carry):
+            origin = (lon + k) % lons
+            to_polar(crecv.at[i, origin], origin)
+            return carry
+
+        lax.fori_loop(1, lons, relay, 0)
+
+    def chunk(i, carry):
+        unit = jnp.where(polar, 0, start) + lon * mine + i
+        plane = unit // EACH
+        row = pl.multiple_of(unit % EACH * PART, PART)
+
+        @pl.when(polar | helper)
+        def _():
+            pltpu.make_async_copy(recv.at[i], recv.at[i], rsem.at[i]).wait()
+            transform(i, base + row, recv, ybuf, cut_ref, cutb, tw_ref, wv, terms, acc)
+
+        @pl.when(polar)
+        def _():
+            target = filt.at[plane, pl.ds(row, PART), :]
+            pltpu.make_async_copy(ybuf.at[i, lon], target, fsem).start()
+
+            def back(k, carry):
+                to = (lon + k) % lons
+                pltpu.make_async_remote_copy(ybuf.at[i, to], target, csend, fsem, device_id=peer(0, to), device_id_type=MESH).start()
+                return carry
+
+            lax.fori_loop(1, lons, back, 0)
+
+            @pl.when(i + AHEAD < TAKES[0])
+            def _():
+                deal_near(i + AHEAD)
+
+        @pl.when(helper)
+        def _():
+            def swap(k, carry):
+                to = (lon + k) % lons
                 pltpu.make_async_remote_copy(
-                    f_ref.at[plane, rows, :], recv.at[i, lon], osem.at[i], rsem.at[i], device_id=peer(xm_to, to), device_id_type=MESH
+                    ybuf.at[i, to], crecv.at[i, lon], csend, crsem.at[i], device_id=peer(xm, to), device_id_type=MESH
                 ).start()
-
-            if i < TAKES[1]:
-                send(1)
-                send(3)
-
-            @pl.when(k > 0)
-            def _():
-                send(0)
-
-            return carry
-
-        lax.fori_loop(0, lons, one, 0)
-
-    @pl.when(polar)
-    def _():
-        for i in range(AHEAD):
-            deal(i)
+                return carry
+
+            lax.fori_loop(1, lons, swap, 0)
+
+        @pl.when(helper & (i >= LAG))
+        def _():
+            forward(i - LAG)
+
+        return carry
+
+    lax.fori_loop(0, mine, chunk, 0)
+
+    @pl.when(helper)
+    def _():
+        for i in range(LAG):
+            forward(mine - LAG + i)
 
     for copy in first:
         copy.wait_recv()
@@ -331,103 +416,23 @@
             state[2, rows, :] = masks[2, rows, :] * (state[2, rows, :] - COEF * (below - s))
         return carry
 
-    for copy in tables:
-        copy.wait()
-
-    base = ylo * 128 + core * ROWS
-    far = xm // 2
-    start = STARTS[1] + (STARTS[3] - STARTS[1]) * far
-
-    def forward(i):
-        pltpu.make_async_copy(crecv.at[0, pl.ds(0, 7)], crecv.at[0, pl.ds(0, 7)], crsem.at[i]).wait()
-
-        def to_polar(source, origin):
-            unit = start + origin * TAKES[1] + i
-            rows = pl.ds(pl.multiple_of(unit % EACH * PART, PART), PART)
-            pltpu.make_async_remote_copy(
-                source, filt.at[unit // EACH, rows, :], dsend, fsem, device_id=peer(0, lon), device_id_type=MESH
-            ).start()
-
-        to_polar(ybuf.at[i, lon], lon)
-
-        def relay(k, carry):
-            origin = (lon + k) % lons
-            to_polar(crecv.at[i, origin], origin)
-            return carry
-
-        lax.fori_loop(1, lons, relay, 0)
-
-    @pl.when(polar)
-    def _():
-        for i in range(2):
-            settle(i)
-            deal(i + AHEAD)
-
-    def chunk(i, carry):
-        unit = jnp.where(polar, lon * TAKES[0], start + lon * TAKES[1]) + i
-        plane = unit // EACH
-        row = pl.multiple_of(unit % EACH * PART, PART)
-
-        @pl.when(polar | helper)
-        def _():
-            pltpu.make_async_copy(recv.at[i], recv.at[i], rsem.at[i]).wait()
-            transform(i, base + row, recv, ybuf, cut_ref, cutb, tw_ref, wv, terms, acc)
-
-        @pl.when(polar)
-        def _():
-            target = filt.at[plane, pl.ds(row, PART), :]
-            pltpu.make_async_copy(ybuf.at[i, lon], target, fsem).start()
-
-            def back(k, carry):
-                to = (lon + k) % lons
-                pltpu.make_async_remote_copy(ybuf.at[i, to], target, csend, fsem, device_id=peer(0, to), device_id_type=MESH).start()
-                return carry
-
-            lax.fori_loop(1, lons, back, 0)
-            for g in range(TAKES[0] - AHEAD - 2):
-
-                @pl.when(i == g)
-                def _():
-                    settle(g + 2)
-                    deal(g + 2 + AHEAD)
-
-        @pl.when(helper)
-        def _():
-            def swap(k, carry):
-                to = (lon + k) % lons
-                pltpu.make_async_remote_copy(
-                    ybuf.at[i, to], crecv.at[i, lon], csend, crsem.at[i], device_id=peer(xm, to), device_id_type=MESH
-                ).start()
-                return carry
-
-            lax.fori_loop(1, lons, swap, 0)
-
-        lax.fori_loop(0, jnp.where(i < TAKES[1], SUB // TAKES[1], 0) + jnp.where(i < SUB % TAKES[1], 1, 0), cycle, 0)
-
-        @pl.when(helper & (i >= LAG))
-        def _():
-            forward(i - LAG)
-
-        return carry
-
-    lax.fori_loop(0, jnp.where(polar, TAKES[0], TAKES[1]), chunk, 0)
+    lax.fori_loop(0, SUB, cycle, 0)
     held_flow[...] = state[:, pl.ds(HALO, ROWS), 0:COLS]
     held_opens[...] = masks[1:3, pl.ds(HALO, ROWS), 0:COLS]
     made = [pltpu.make_async_copy(held_flow, flow, wsem.at[0]), pltpu.make_async_copy(held_opens, opens, wsem.at[1])]
     for copy in made:
         copy.start()
 
-    @pl.when(helper)
-    def _():
-        for i in range(TAKES[1] - LAG, TAKES[1]):
-            forward(i)
-        drain(7 * TAKES[1], csend)
-        drain(8 * TAKES[1], dsend)
+    for side in (1, 3):
+
+        @pl.when(xm == side)
+        def _():
+            drain(7 * TAKES[side], csend)
+            drain(8 * TAKES[side], dsend)
 
     @pl.when(polar)
     def _():
-        for i in range(TAKES[0] - AHEAD, TAKES[0]):
-            settle(i)
+        drain(7 * TAKES[0] + 8 * TAKES[1] + 8 * TAKES[3], osem)
         drain(7 * TAKES[0], csend)
         drain(32 * EACH, fsem)
 
@@ -528,7 +533,7 @@
             pltpu.VMEM((3, ROWS, COLS), f32),
             pltpu.VMEM((2, ROWS, COLS), f32),
             *strips,
-            dma((5,)), dma((16,)), dma((16,)), dma((TAKES[0],)), dma((TAKES[0],)), dma, dma((TAKES[1],)), dma, dma,
+            dma((5,)), dma((16,)), dma((16,)), dma((TAKES[0],)), dma, dma, dma((TAKES[1],)), dma, dma,
         ],
         compiler_params=pltpu.CompilerParams(collective_id=1, has_side_effects=True, vmem_limit_bytes=67043328),
     )(planes, barotropic, land_sea, cutoff, jnp.asarray(table), jnp.asarray(twist))

time: 69.2 us -> 66.2 us (0.957)
  Pallas kernels: 68.5 us -> 65.3 us
    pallas_call x1, Pallas kernels: 63.8 us -> 60.6 us  [body(): pl.pallas_call(exchange_kernel, out_shape=(jax.ShapeDtypeStruct((32, ROWS...]
where the time goes in v3:
time: 66.2 us; the launch traced here: 65.9 us
  Pallas kernels  65.3 us (99%)
    pallas_call x1, Pallas kernels, body(): pl.pallas_call(exchange_kernel, out_shape=(jax.ShapeDtypeStruct((32, ROWS...  60.6 us
    pallas_call x1, Pallas kernels, body(): pl.pallas_call(finish_kernel, out_shape=(jax.ShapeDtypeStruct((16, ROWS,...  4.74 us

profile of v3, /device:TPU:1, one launch (start us, length us, event | category | flops | bytes accessed | tf_op | source)
XLA Modules:
  0.0 65.9 jit_solution(11923599232028561982)
XLA Ops:
  0.6 60.6 %shard_map.94 = (f32[32,64,450]{2,1,0:T(8,128)}, f32[3,64,450]{2,1,0:T(8,128)}, f32[2,64,450]{2,1,0:T(8,128)}) custom-call(f32[32,64,450]{2,1,0:T(8,128)} %bitcast.3, f32[3,64,450]{2,1,0:T(8,128)} %baro_in.1, s32[64,450]{1,0:T(8,128)} %land_in.1, s32[256]{0:T(256)} %cut_in.1, bf16[2,512,1024]{2,1,0:T(8,128)(2,1)} %constant.4.clone.w_ref, ...), custom_call_target="tpu_custom_call" | custom-call | tf_op jit(solution)/shard_map/pallas_call | solution.py:509
  61.2 4.7 %shard_map.95 = (f32[16,64,450]{2,1,0:T(8,128)}, f32[16,64,450]{2,1,0:T(8,128)}, f32[64,450]{1,0:T(8,128)}) custom-call(f32[8]{0:T(128)} %thick_in.1, f32[32,64,450]{2,1,0:T(8,128)} %bitcast.4, f32[32,64,450]{2,1,0:T(8,128)} %get-tuple-element.9.filt, f32[3,64,450]{2,1,0:T(8,128)} %get-tuple-element.10.flow_in, f32[2,64,450]{2,1,0:T(8,128)} %get-tuple-element.11.opens_in), custom_call_target="tpu_custom_call" | custom-call | tf_op jit(solution)/shard_map/pallas_call | solution.py:540

commit v4 on v3

--- a/solution.py
+++ b/solution.py
@@ -21,8 +21,8 @@
 EACH = ROWS // PART
 TAKES = (13, 10, 0, 9)
 STARTS = (0, 104, 184, 184)
-LAG = 2
-AHEAD = 6
+LAG = 3
+AHEAD = 13
 HALO = 24
 TILES = ((0, 128), (128, 256), (256, 384), (384, 450))
 ROOT = math.sqrt(0.5)

time: 66.2 us -> 66 us (level)
  no operation moved by 1% of the time
where the time goes in v4:
time: 66 us; the launch traced here: 65.9 us
  Pallas kernels  65.3 us (99%)
    pallas_call x1, Pallas kernels, body(): pl.pallas_call(exchange_kernel, out_shape=(jax.ShapeDtypeStruct((32, ROWS...  60.6 us
    pallas_call x1, Pallas kernels, body(): pl.pallas_call(finish_kernel, out_shape=(jax.ShapeDtypeStruct((16, ROWS,...  4.74 us

profile of v4, /device:TPU:1, one launch (start us, length us, event | category | flops | bytes accessed | tf_op | source)
XLA Modules:
  0.0 65.9 jit_solution(17533715337034939055)
XLA Ops:
  0.6 60.6 %shard_map.94 = (f32[32,64,450]{2,1,0:T(8,128)}, f32[3,64,450]{2,1,0:T(8,128)}, f32[2,64,450]{2,1,0:T(8,128)}) custom-call(f32[32,64,450]{2,1,0:T(8,128)} %bitcast.3, f32[3,64,450]{2,1,0:T(8,128)} %baro_in.1, s32[64,450]{1,0:T(8,128)} %land_in.1, s32[256]{0:T(256)} %cut_in.1, bf16[2,512,1024]{2,1,0:T(8,128)(2,1)} %constant.4.clone.w_ref, ...), custom_call_target="tpu_custom_call" | custom-call | tf_op jit(solution)/shard_map/pallas_call | solution.py:509
  61.2 4.7 %shard_map.95 = (f32[16,64,450]{2,1,0:T(8,128)}, f32[16,64,450]{2,1,0:T(8,128)}, f32[64,450]{1,0:T(8,128)}) custom-call(f32[8]{0:T(128)} %thick_in.1, f32[32,64,450]{2,1,0:T(8,128)} %bitcast.4, f32[32,64,450]{2,1,0:T(8,128)} %get-tuple-element.9.filt, f32[3,64,450]{2,1,0:T(8,128)} %get-tuple-element.10.flow_in, f32[2,64,450]{2,1,0:T(8,128)} %get-tuple-element.11.opens_in), custom_call_target="tpu_custom_call" | custom-call | tf_op jit(solution)/shard_map/pallas_call | solution.py:540
